TPU v7x, 32 devices: a whole 2x2x4 slice. The times are simulated.
32 devices in a mesh: wide: 8 (over z, x), narrow: 4 (over y, core).
Axes of the slice: x: 2, y: 2, z: 4, core: 2. Of those that a mesh axis runs over, the one named last changes fastest.
Arguments:
- harvest: bfloat16 [128, 16384], P('wide', 'narrow'), may hold values from -6 to 6
- pair_ids: int32 [16], P('wide'), may hold values from 0 to 15
- w_enc: bfloat16 [16384, 32768], P('narrow', 'wide'), may hold values from -0.046875 to 0.046875
- b_enc: float32 [32768], P('wide'), may hold values from -3 to 3
- w_dec: bfloat16 [32768, 16384], P('wide', 'narrow'), may hold values from -0.03125 to 0.03125
- b_dec: float32 [16384], P('narrow'), may hold values from -3 to 3
- step_size: float32 [], replicated, may hold values from 0.1 to 0.33
- penalty: float32 [], replicated, may hold values from 0.5 to 2
Outputs:
- latents: float32 [16, 32768], P(None, 'wide')
Inputs may be any that keep to these rules, and one draw needn't show every extreme that they name: Token pair b takes pool row (b // 2) * 16 + pair_ids[b].
All inputs are finite; a program needn't handle non-finite values.
Results may differ from a plain program's by a relative error of at most 0.0025.
Values may be sent and summed in bfloat16 or wider, within the bound.
No kernel may reach another device: no remote copies, remote signals or barrier semaphores. Data moves between devices by JAX's collectives and lax.ppermute only.
A program may use at most 128 MiB of HBM per device.

v0:
```python
import jax
import jax.numpy as jnp
from jax import lax
from jax.sharding import PartitionSpec as P

ITERS = 2


def transpose_product(left, weights):
    return lax.dot_general(
        left, weights, (((1,), (1,)), ((), ())), preferred_element_type=jnp.float32
    )


def local(harvest, pair_ids, w_enc, b_enc, w_dec, b_dec, step_size, penalty):
    pool_rows = harvest.shape[0]
    chooser = (pair_ids[:, None] == jnp.arange(pool_rows, dtype=jnp.int32)[None, :]).astype(
        jnp.bfloat16
    )
    own_pairs = jnp.dot(chooser, harvest, preferred_element_type=jnp.float32).astype(jnp.bfloat16)
    squares = jnp.einsum("ld,ld->l", w_dec, w_dec, preferred_element_type=jnp.float32)
    first_half = lax.axis_index("narrow") < lax.axis_size("narrow") // 2
    square_base = jnp.where(first_half, squares, 0.0)
    square_inst = jnp.where(first_half, 0.0, squares)
    all_pairs = lax.all_gather(own_pairs, "wide", axis=0, tiled=True)
    pre_part = jnp.dot(all_pairs, w_enc, preferred_element_type=jnp.float32)
    pre, total_base, total_inst = lax.psum((pre_part, square_base, square_inst), "narrow")
    thresh = penalty * step_size * (jnp.sqrt(total_base) + jnp.sqrt(total_inst))
    latents = jnp.maximum(pre + b_enc, 0.0)
    for step in range(ITERS):
        code_bf = latents.astype(jnp.bfloat16)
        rebuilt = lax.psum(jnp.dot(code_bf, w_dec, preferred_element_type=jnp.float32), "wide")
        residual = (all_pairs.astype(jnp.float32) - rebuilt - b_dec).astype(jnp.bfloat16)
        grad_part = transpose_product(residual, w_dec)
        grad = lax.psum(grad_part, "narrow")
        latents = jnp.maximum(latents + step_size * grad - thresh, 0.0)
    return latents


def solution(mesh):
    return jax.shard_map(
        local,
        mesh=mesh,
        in_specs=(
            P("wide", "narrow"),
            P("wide"),
            P("narrow", "wide"),
            P("wide"),
            P("wide", "narrow"),
            P("narrow"),
            P(),
            P(),
        ),
        out_specs=P(None, "wide"),
        check_vma=False,
    )
```

profile of v0, /device:TPU:0, one launch (start us, length us, event | category | flops | bytes accessed | tf_op | source)
XLA Modules:
  0.0 363.5 jit_solution(2875253534670136173)
XLA Ops:
  6.5 0.0 copy-start
  6.5 0.0 copy-start.4
  6.5 0.0 all-reduce.7.cloned.1.call-start
  6.5 0.9 copy-done
  7.4 0.9 fusion.1
  8.3 32.3 %all-gather = bf16[8,2,4096]{2,1,0:T(2,128)(2,1)S(1)} all-gather(bf16[1,2,4096]{2,1,0:T(2,128)(2,1)S(1)} %fusion.1), channel_id=1, replica_groups=mesh['wide'=8,'narrow'=4] {'wide'}, dimensions={0}, use_global_device_ids=true | all-gather | bytes 147456 | tf_op jit(solution)/shard_map/all_gather | solution.py:25
  40.6 0.1 reshape.5
  40.7 13.5 %fusion.24 = f32[16,4096]{1,0:T(8,128)} fusion(bf16[16,4096]{1,0:T(8,128)(2,1)S(1)} %reshape.5, bf16[4096,4096]{1,0:T(8,128)(2,1)} %param.10), kind=kOutput, calls=%fused_computation.31 | convolution fusion | flops 536870912 | bytes 33947648 | tf_op jit(solution)/shard_map/dot_general | solution.py:26
  54.2 0.0 all-reduce.7.cloned.1.call-update
  54.3 0.0 copy-start.5
  54.3 0.0 all-reduce.9.cloned.1.call-start
  54.3 33.3 %all-reduce.7.cloned.1.call-done = f32[16,4096]{1,0:T(8,128)} async-done(((f32[16,4096]{1,0:T(8,128)}), f32[16,4096]{1,0:T(8,128)}) %all-reduce.7.cloned.1.call-update) | async-done | bytes 262160 | tf_op jit(solution)/shard_map/psum | solution.py:27
  87.6 0.0 copy-done.4
  87.6 15.8 %fusion.7 = f32[16,4096]{1,0:T(8,128)} fusion(bf16[4096,4096]{1,0:T(8,128)(2,1)} %param.12, f32[16,4096]{1,0:T(8,128)} %all-reduce.7.cloned.1.call-done, f32[4096]{0:T(1024)S(1)} %copy-done.4), kind=kOutput, calls=%fused_computation.14 | convolution fusion | flops 537067520 | bytes 34095104 | tf_op jit(solution)/shard_map/dot_general | solution.py:32
  103.4 0.0 all-reduce.9.cloned.1.call-update
  103.4 0.0 copy-start.2
  103.4 0.0 all-reduce.11.cloned.1.call-start
  103.5 11.5 %fusion = f32[4096]{0:T(1024)S(1)} fusion(bf16[4096,4096]{1,0:T(8,128)(2,1)} %param.12), kind=kLoop, calls=%fused_computation.1 | loop fusion | flops 50327552 | bytes 33570816 | tf_op jit(solution)/shard_map/ld,ld->l/dot_general | solution.py:21
  116.2 10.7 %all-reduce = (f32[4096]{0:T(1024)S(1)}, f32[4096]{0:T(1024)S(1)}) all-reduce(f32[4096]{0:T(1024)S(1)} %get-tuple-element.8, f32[4096]{0:T(1024)S(1)} %get-tuple-element.7), channel_id=1, replica_groups=mesh['wide'=8,'narrow'=4] {'narrow'}, use_global_device_ids=true, to_apply=%region_4.5 | all-reduce | flops 8192 | bytes 65536 | tf_op jit(solution)/shard_map/psum | solution.py:27
  126.9 47.6 %all-reduce.9.cloned.1.call-done = f32[16,4096]{1,0:T(8,128)} async-done(((f32[16,4096]{1,0:T(8,128)}), f32[16,4096]{1,0:T(8,128)}) %all-reduce.9.cloned.1.call-update) | async-done | bytes 262160 | tf_op jit(solution)/shard_map/psum | solution.py:32
  174.6 0.0 copy-done.5
  174.6 15.2 %fusion.11 = f32[16,4096]{1,0:T(8,128)} fusion(bf16[4096,4096]{1,0:T(8,128)(2,1)} %param.12, f32[16,4096]{1,0:T(8,128)} %all-reduce.9.cloned.1.call-done, bf16[16,4096]{1,0:T(8,128)(2,1)S(1)} %reshape.5, f32[4096]{0:T(1024)S(1)} %copy-done.5), kind=kOutput, calls=%fused_computation.16 | convolution fusion | flops 537133056 | bytes 34226176 | tf_op jit(solution)/shard_map/dot_general | solution.py:10
  189.8 0.0 all-reduce.11.cloned.1.call-update
  189.8 0.2 all-reduce.13.cloned.1.call-start
  190.0 0.0 copy-start.1
  190.0 31.4 %all-reduce.11.cloned.1.call-done = f32[16,4096]{1,0:T(8,128)} async-done(((f32[16,4096]{1,0:T(8,128)}), f32[16,4096]{1,0:T(8,128)}) %all-reduce.11.cloned.1.call-update) | async-done | bytes 262160 | tf_op jit(solution)/shard_map/psum | solution.py:35
  221.4 0.0 copy-done.2
  221.4 0.0 copy-start.3
  221.4 15.8 %fusion.13 = f32[16,4096]{1,0:T(8,128)} fusion(bf16[4096,4096]{1,0:T(8,128)(2,1)} %param.12, f32[16,4096]{1,0:T(8,128)} %all-reduce.11.cloned.1.call-done, f32[16,4096]{1,0:T(8,128)S(1)} %copy-done.2, f32[4096]{0:T(1024)S(1)} %add_multiply_fusion, f32[]{:T(128)S(6)} %copy.18, f32[4096]{0:T(1024)S(1)} %copy-done.4), kind=kOutput, calls=%fused_computation.17 | convolution fusion | flops 537329664 | bytes 34373636 | tf_op jit(solution)/shard_map/dot_general | solution.py:32
  237.2 0.0 all-reduce.13.cloned.1.call-update
  237.3 0.0 all-reduce.15.cloned.1.call-start
  237.3 71.1 %all-reduce.13.cloned.1.call-done = f32[16,4096]{1,0:T(8,128)} async-done(((f32[16,4096]{1,0:T(8,128)}), f32[16,4096]{1,0:T(8,128)}) %all-reduce.13.cloned.1.call-update) | async-done | bytes 262160 | tf_op jit(solution)/shard_map/psum | solution.py:32
  308.4 15.2 %fusion.9 = f32[16,4096]{1,0:T(8,128)} fusion(bf16[4096,4096]{1,0:T(8,128)(2,1)} %param.12, f32[16,4096]{1,0:T(8,128)} %all-reduce.13.cloned.1.call-done, bf16[16,4096]{1,0:T(8,128)(2,1)S(1)} %reshape.5, f32[4096]{0:T(1024)S(1)} %copy-done.5), kind=kOutput, calls=%fused_computation.15 | convolution fusion | flops 537133056 | bytes 34226176 | tf_op jit(solution)/shard_map/dot_general | solution.py:10
  323.6 0.0 all-reduce.15.cloned.1.call-update
  323.6 31.6 %all-reduce.15.cloned.1.call-done = f32[16,4096]{1,0:T(8,128)} async-done(((f32[16,4096]{1,0:T(8,128)}), f32[16,4096]{1,0:T(8,128)}) %all-reduce.15.cloned.1.call-update) | async-done | bytes 262160 | tf_op jit(solution)/shard_map/psum | solution.py:35
  355.3 0.0 copy-done.3
  355.3 1.7 subtract_maximum_fusion
  357.0 0.0 copy-done.1
  (2 shorter events, 0.0 us)
Async XLA Ops:
  6.5 0.9 copy-start
  6.5 81.1 %copy-start.4 = (f32[4096]{0:T(1024)S(1)}, f32[4096]{0:T(1024)}, u32[]{:S(2)}) copy-start(f32[4096]{0:T(1024)} %param.11) | copy-start | bytes 49156
  6.5 81.1 %all-reduce.7.cloned.1.call-start = ((), (), s32[]{:S(2)}) async-start(), calls=%async_computation | async-start | bytes 524288 | tf_op jit(solution)/shard_map/psum | solution.py:27
  54.3 120.3 %copy-start.5 = (f32[4096]{0:T(1024)S(1)}, f32[4096]{0:T(1024)}, u32[]{:S(2)}) copy-start(f32[4096]{0:T(1024)} %param.13) | copy-start | bytes 49156
  54.3 120.3 %all-reduce.9.cloned.1.call-start = ((), (), s32[]{:S(2)}) async-start(), calls=%async_computation.1 | async-start | bytes 524288 | tf_op jit(solution)/shard_map/psum | solution.py:32
  103.4 118.0 %copy-start.2 = (f32[16,4096]{1,0:T(8,128)S(1)}, f32[16,4096]{1,0:T(8,128)}, u32[]{:S(2)}) copy-start(f32[16,4096]{1,0:T(8,128)} %all-reduce.7.cloned.1.call-done) | copy-start | bytes 786436
  103.4 118.0 %all-reduce.11.cloned.1.call-start = ((), (), s32[]{:S(2)}) async-start(), calls=%async_computation.2 | async-start | bytes 524288 | tf_op jit(solution)/shard_map/psum | solution.py:35
  189.8 118.7 %all-reduce.13.cloned.1.call-start = ((), (), s32[]{:S(2)}) async-start(), calls=%async_computation.3 | async-start | bytes 524288 | tf_op jit(solution)/shard_map/psum | solution.py:32
  190.0 167.0 %copy-start.1 = (bf16[16,4096]{1,0:T(8,128)(2,1)S(1)}, bf16[16,4096]{1,0:T(8,128)(2,1)}, u32[]{:S(2)}) copy-start(bf16[16,4096]{1,0:T(8,128)(2,1)} %param.8) | copy-start | bytes 393220
  221.4 133.8 %copy-start.3 = (f32[16,4096]{1,0:T(8,128)S(1)}, f32[16,4096]{1,0:T(8,128)}, u32[]{:S(2)}) copy-start(f32[16,4096]{1,0:T(8,128)} %all-reduce.11.cloned.1.call-done) | copy-start | bytes 786436
  237.3 118.0 %all-reduce.15.cloned.1.call-start = ((), (), s32[]{:S(2)}) async-start(), calls=%async_computation.4 | async-start | bytes 524288 | tf_op jit(solution)/shard_map/psum | solution.py:35
Sparse Core Ops, SparseCore 0:
  54.4 33.1 all-reduce.6
  103.5 70.9 all-reduce.8
  189.9 31.4 all-reduce.10
  237.4 70.9 all-reduce.12
  323.7 31.4 all-reduce.14
where the time goes:
time: 364 us
  waiting for transfers between devices  215 us (59%)
  matrix products  76.4 us (21%)
  blocking collectives  43 us (12%)
  between operations  14.5 us (4%)
  other arithmetic  13.2 us (4%)
    psum x2, waiting for transfers between devices, local(): lax.psum(jnp.dot(code_bf, w_dec, preferred_element_type=jnp.float32), 'wi...  119 us
    psum x2, waiting for transfers between devices, local(): grad = lax.psum(grad_part, 'narrow')  63 us
    psum x1, waiting for transfers between devices, local(): lax.psum((pre_part, square_base, square_inst), 'narrow')  33.3 us
    all_gather x1, blocking collectives, local(): all_pairs = lax.all_gather(own_pairs, 'wide', axis=0, tiled=True)  32.3 us
    dot_general x2, matrix products, local(): jnp.dot(code_bf, w_dec, preferred_element_type=jnp.float32)  31.6 us
    dot_general x2, matrix products, transpose_product(): lax.dot_general(left, weights, (((1,), (1,)), ((), ())), preferred_elemen...  30.3 us
    dot_general x1, matrix products, local(): pre_part = jnp.dot(all_pairs, w_enc, preferred_element_type=jnp.float32)  13.5 us
    dot_general x1, other arithmetic, local(): jnp.einsum('ld,ld->l', w_dec, w_dec, preferred_element_type=jnp.float32)  11.5 us
  transfers between devices with their start and end apart: 5, of which 5 were waited for; matrix products, arithmetic and copies ran while one was open for 3% of the time, Pallas kernels for 0%

commit v1 on v0

v1 whole, which is shorter than its diff:
```python
import functools

import jax
import jax.numpy as jnp
from jax import lax
from jax.experimental import pallas as pl
from jax.experimental.pallas import tpu as pltpu
from jax.sharding import PartitionSpec as P

ITERS = 2
MIB = 1024 * 1024
F32 = jnp.float32
BF16 = jnp.bfloat16
NT = (((1,), (1,)), ((), ()))


def swap(value, axis, distance):
    pairs = [(i, i ^ distance) for i in range(lax.axis_size(axis))]
    return lax.ppermute(value, axis, pairs)


def bits_of(axis):
    size = lax.axis_size(axis)
    assert size & (size - 1) == 0
    return [1 << k for k in range(size.bit_length() - 1)]


def tile_of(length, most):
    size = most
    while length % size:
        size //= 2
    return size


def half_start(axis, bit, half, other):
    high = jnp.where((lax.axis_index(axis) & bit) != 0, 1, 0)
    start = (1 - high if other else high) * half
    return pl.multiple_of(start, half)


def local_call(body, name, arrays, outs, flops, scalars=(), scratch=(), vmem=16, in_hbm=(), traffic=None):
    specs = [pl.BlockSpec(memory_space=pltpu.SMEM)] * len(scalars)
    specs += [pl.BlockSpec(memory_space=pltpu.HBM if k in in_hbm else pltpu.VMEM) for k in range(len(arrays))]
    multiple = isinstance(outs, (list, tuple))
    out_spec = pl.BlockSpec(memory_space=pltpu.VMEM)
    return pl.pallas_call(
        body,
        out_shape=outs,
        in_specs=specs,
        out_specs=[out_spec] * len(outs) if multiple else out_spec,
        scratch_shapes=list(scratch),
        compiler_params=pltpu.CompilerParams(vmem_limit_bytes=vmem * MIB),
        cost_estimate=pl.CostEstimate(flops=flops, bytes_accessed=flops // 32 if traffic is None else traffic, transcendentals=0),
        name=name,
    )(*scalars, *arrays)


def select(harvest, pair_ids, step_size, penalty, half_lat, w_enc):
    pool, feat = harvest.shape
    rows = pair_ids.shape[0]

    def body(step_ref, pen_ref, ids_ref, pool_ref, _, o_ref, step_row, pen_row):
        row = lax.broadcasted_iota(jnp.int32, (rows, pool), 0)
        col = lax.broadcasted_iota(jnp.int32, (rows, pool), 1)
        taken = jnp.zeros((rows, pool), F32)
        for r in range(rows):
            taken = jnp.where((row == r) & (col == ids_ref[r]), 1.0, taken)
        taken = taken.astype(BF16)
        chunk = tile_of(feat, 1024)

        @pl.loop(0, feat // chunk)
        def _(j):
            here = pl.ds(pl.multiple_of(j * chunk, chunk), chunk)
            o_ref[:, here] = jnp.dot(taken, pool_ref[:, here], preferred_element_type=F32).astype(BF16)

        step_row[...] = jnp.full((1, half_lat), step_ref[0, 0], F32)
        pen_row[...] = jnp.full((1, half_lat), pen_ref[0, 0] * step_ref[0, 0], F32)

    outs = [
        jax.ShapeDtypeStruct((rows, feat), BF16),
        jax.ShapeDtypeStruct((1, half_lat), F32),
        jax.ShapeDtypeStruct((1, half_lat), F32),
    ]
    scalars = [step_size.reshape(1, 1), penalty.reshape(1, 1), pair_ids]
    return local_call(body, "select", [harvest, w_enc], outs, 1 << 20, scalars, vmem=4, in_hbm=(1,))


def merge(mine, other, w_enc):
    count, feat = mine.shape

    def body(mine_ref, other_ref, _, o_ref):
        both = jnp.concatenate([mine_ref[...].astype(F32), other_ref[...].astype(F32)])
        o_ref[...] = both.astype(BF16)

    out = jax.ShapeDtypeStruct((2 * count, feat), BF16)
    return local_call(body, "merge", [mine, other, w_enc], out, 1 << 20, vmem=4, in_hbm=(2,))


def hold(w_dec, after):
    def body(w_ref, after_ref, o_ref):
        o_ref[...] = jnp.zeros(o_ref.shape, F32)

    out = jax.ShapeDtypeStruct((8, 128), F32)
    return local_call(body, "hold", [w_dec, pltpu.with_memory_space_constraint(after, pltpu.HBM)], out, 1 << 10, in_hbm=(1,))


def order(mine, other, b_enc, b_dec, step_row, pen_row, held, rows, far, hidden):
    count, feat = mine.shape
    half_feat, half_lat = feat // 2, b_enc.shape[1] // 2

    def body(mine_ref, other_ref, b_enc_ref, b_dec_ref, step_ref, pen_ref, _, all_ref, own_ref, enc_ref, dec_ref, step_out, pen_out):
        me = lax.axis_index("wide")
        row = lax.broadcasted_iota(jnp.int32, (2 * count, count), 0)
        col = lax.broadcasted_iota(jnp.int32, (2 * count, count), 1)

        def place(base):
            at = col + base
            return (row == rows * (me ^ (at // rows)) + at % rows).astype(F32).astype(BF16)

        chunk = tile_of(half_feat, 1024)
        start = half_start("wide", hidden, half_feat, False)

        @pl.loop(0, feat // chunk)
        def _(j):
            here = pl.ds(pl.multiple_of(j * chunk, chunk), chunk)
            both = jnp.dot(place(0), mine_ref[:, here], preferred_element_type=F32)
            both = both + jnp.dot(place(count), other_ref[:, here], preferred_element_type=F32)
            all_ref[:, here] = both.astype(BF16)

        own_ref[...] = all_ref[:, pl.ds(start, half_feat)]
        dec_ref[...] = b_dec_ref[:, pl.ds(start, half_feat)]
        enc_ref[...] = b_enc_ref[:, pl.ds(half_start("narrow", far, half_lat, False), half_lat)]
        step_out[...] = step_ref[...]
        pen_out[...] = pen_ref[...]

    outs = [
        jax.ShapeDtypeStruct((2 * count, feat), BF16),
        jax.ShapeDtypeStruct((2 * count, half_feat), BF16),
        jax.ShapeDtypeStruct((1, half_lat), F32),
        jax.ShapeDtypeStruct((1, half_feat), F32),
        jax.ShapeDtypeStruct((1, half_lat), F32),
        jax.ShapeDtypeStruct((1, half_lat), F32),
    ]
    return local_call(body, "order", [mine, other, b_enc, b_dec, step_row, pen_row, held], outs, 1 << 20, vmem=4)


def pointwise(fn, name, arrays, outs, w_dec):
    def body(*refs):
        ins, out_refs = refs[:len(arrays)], refs[len(arrays) + 1:]
        values = fn(*(ref[...] for ref in ins))
        for ref, value in zip(out_refs, values, strict=True):
            ref[...] = value

    return local_call(body, name, [*arrays, w_dec], outs, 1 << 16)


def encode(x, w, far, other, name):
    depth, lat = w.shape
    half = lat // 2
    chunk = tile_of(depth, 512)
    steps = depth // chunk
    slots = min(4, steps)

    def body(x_ref, w_ref, o_ref, held, sems):
        start = half_start("narrow", far, half, other)

        def fetch(k):
            return pltpu.make_async_copy(
                w_ref.at[pl.ds(k * chunk, chunk), pl.ds(start, half)], held.at[k % slots], sems.at[k % slots]
            )

        for k in range(slots):
            fetch(k).start()
        for k in range(steps):
            fetch(k).wait()
            width = tile_of(half, 1024)

            @pl.loop(0, half // width)
            def _(j):
                here = pl.ds(pl.multiple_of(j * width, width), width)
                part = jnp.dot(x_ref[:, k * chunk:(k + 1) * chunk], held[k % slots, :, here], preferred_element_type=F32)
                if k:
                    part = part + o_ref[:, here]
                o_ref[:, here] = part

            if k + slots < steps:
                fetch(k + slots).start()

    out = jax.ShapeDtypeStruct((x.shape[0], half), F32)
    scratch = [pltpu.VMEM((slots, chunk, half), BF16), pltpu.SemaphoreType.DMA((slots,))]
    return local_call(body, name, [x, w], out, 2 * x.shape[0] * depth * half, scratch=scratch, vmem=12, in_hbm=(1,))


def product(x, w, acc, dtype, depth_at, width_at, transposed, name):
    depth = x.shape[1]
    width = w.shape[0 if transposed else 1]
    if width_at is not None:
        width //= 2
    step = tile_of(width, 1024)

    def body(x_ref, w_ref, *rest):
        *acc_ref, o_ref = rest
        deep = pl.ds(half_start(*depth_at[:2], depth, depth_at[2]), depth)
        base = 0 if width_at is None else half_start(*width_at[:2], width, width_at[2])

        @pl.loop(0, width // step)
        def _(j):
            there = pl.ds(pl.multiple_of(base + j * step, step), step)
            here = pl.ds(pl.multiple_of(j * step, step), step)
            if transposed:
                part = lax.dot_general(x_ref[...], w_ref[there, deep], NT, preferred_element_type=F32)
            else:
                part = jnp.dot(x_ref[...], w_ref[deep, there], preferred_element_type=F32)
            if acc_ref:
                part = part + acc_ref[0][:, there]
            o_ref[:, here] = part.astype(dtype)

    out = jax.ShapeDtypeStruct((x.shape[0], width), dtype)
    arrays = [x, w] + ([] if acc is None else [acc])
    return local_call(body, name, arrays, out, 2 * x.shape[0] * depth * width)


def squares_of(w, far):
    rows, cols = w.shape
    half = rows // 2
    step = tile_of(half, 128)

    def body(w_ref, o_ref):
        for other in (False, True):
            start = half_start("narrow", far, half, other)

            @pl.loop(0, half // step)
            def _(j):
                here = pl.multiple_of(j * step, step)
                there = pl.ds(pl.multiple_of(start + here, step), step)
                total = jnp.zeros((step, 128), F32)
                for c in range(cols // 128):
                    part = w_ref[there, c * 128:(c + 1) * 128].astype(F32)
                    total = total + part * part
                o_ref[int(other):int(other) + 1, pl.ds(here, step)] = jnp.sum(total.T, axis=0, keepdims=True)

    out = jax.ShapeDtypeStruct((2, half), F32)
    return local_call(body, "squares", [w], out, 2 * 16 * rows * cols)


def finish(own, other, far):
    half = own.shape[1]

    def body(own_ref, other_ref, o_ref):
        o_ref[:, pl.ds(half_start("narrow", far, half, False), half)] = own_ref[...]
        o_ref[:, pl.ds(half_start("narrow", far, half, True), half)] = other_ref[...]

    out = jax.ShapeDtypeStruct((own.shape[0], 2 * half), F32)
    return local_call(body, "finish", [own, other], out, 1 << 10)


def local(harvest, pair_ids, w_enc, b_enc, w_dec, b_dec, step_size, penalty):
    rows = pair_ids.shape[0]
    lat, feat = w_dec.shape
    wide_bits, narrow_bits = bits_of("wide"), bits_of("narrow")
    far, near = narrow_bits[-1], narrow_bits[:-1]
    hidden, open_bits = wide_bits[0], wide_bits[1:]
    lat_own, lat_other = ("narrow", far, False), ("narrow", far, True)
    feat_own, feat_other = ("wide", hidden, False), ("wide", hidden, True)
    w_dec = pltpu.with_memory_space_constraint(w_dec, pltpu.VMEM)

    w_enc = pltpu.with_memory_space_constraint(w_enc, pltpu.HBM)
    pairs, step_row, pen_row = select(harvest, pair_ids, step_size, penalty, lat // 2, w_enc)
    for bit in wide_bits[:-1]:
        pairs = merge(pairs, swap(pairs, "wide", bit), w_enc)
    held = hold(w_dec, pen_row)
    pairs, pairs_own, b_enc_own, b_dec_own, step_row, pen_row = order(
        pairs, swap(pairs, "wide", wide_bits[-1]), b_enc[None], b_dec[None], step_row, pen_row, held, rows, far, hidden
    )
    batch = pairs.shape[0]
    wide_f32 = jax.ShapeDtypeStruct((batch, lat // 2), F32)
    lat_bf16 = jax.ShapeDtypeStruct((batch, lat // 2), BF16)
    feat_bf16 = jax.ShapeDtypeStruct((batch, feat // 2), BF16)

    def add_near(value, name):
        for bit in near:
            (value,) = pointwise(lambda a, b: (a + b,), name, [value, swap(value, "narrow", bit)], [jax.ShapeDtypeStruct(value.shape, F32)], w_dec)
        return value

    got = swap(encode(pairs, w_enc, far, True, "enc_other"), "narrow", far)
    (pre,) = pointwise(lambda a, b: (a + b,), "pre", [encode(pairs, w_enc, far, False, "enc_own"), got], [wide_f32], w_dec)
    for bit in near[:-1]:
        pre = pre + swap(pre, "narrow", bit)
    last = swap(pre, "narrow", near[-1])

    def first_codes(a, b, bias):
        value = jnp.maximum(a + b + bias, 0.0)
        return value, value.astype(BF16)

    latents, codes = pointwise(first_codes, "latents", [pre, last, b_enc_own], [wide_f32, lat_bf16], w_dec)

    half_row = jax.ShapeDtypeStruct((1, lat // 2), F32)
    two_rows = jax.ShapeDtypeStruct((2, lat // 2), F32)
    norms = squares_of(w_dec, far)
    for bit in near[:-1]:
        (norms,) = pointwise(lambda a, b: (a + b,), "squared", [norms, swap(norms, "narrow", bit)], [two_rows], w_dec)

    def roots(a, b):
        value = jnp.sqrt(a + b)
        return value[:1], value[1:]

    norm_own, norm_other = pointwise(roots, "norms", [norms, swap(norms, "narrow", near[-1])], [half_row, half_row], w_dec)
    norm_got = swap(norm_other, "narrow", far)

    for step in range(ITERS):
        codes_other = swap(codes, "narrow", far)
        acc = product(codes, w_dec, None, F32, lat_own, None, False, f"rebuild_a{step}")
        send = product(codes_other, w_dec, acc, BF16, lat_other, feat_other, False, f"rebuild_b{step}")
        got = swap(send, "wide", hidden)
        mine = product(codes_other, w_dec, acc, F32, lat_other, feat_own, False, f"rebuild_c{step}")
        for bit in open_bits:
            (mine,) = pointwise(lambda a, b: ((a.astype(F32) + b.astype(F32)).astype(BF16),), f"rebuilt{step}", [mine, got], [feat_bf16], w_dec)
            got = swap(mine, "wide", bit)

        def rest(mine, got, own, bias):
            return ((own.astype(F32) - (mine.astype(F32) + got.astype(F32)) - bias).astype(BF16),)

        (residual,) = pointwise(rest, f"residual{step}", [mine, got, pairs_own, b_dec_own], [feat_bf16], w_dec)
        residual_other = swap(residual, "wide", hidden)
        acc = product(residual, w_dec, None, F32, feat_own, None, True, f"grad_a{step}")
        send = product(residual_other, w_dec, acc, BF16, feat_other, lat_other, True, f"grad_b{step}")
        got = swap(send, "narrow", far)
        grad = product(residual_other, w_dec, acc, F32, feat_other, lat_own, True, f"grad_c{step}")
        for bit in near:
            (grad,) = pointwise(lambda a, b: (a + b.astype(F32),), f"grad{step}", [grad, got], [wide_f32], w_dec)
            got = swap(grad, "narrow", bit)

        def update(latents, grad, got, step_row, pen_row, norm_a, norm_b):
            thresh = pen_row * (norm_a + norm_b)
            value = jnp.maximum(latents + step_row * (grad + got.astype(F32)) - thresh, 0.0)
            return value, value.astype(BF16)

        latents, codes = pointwise(update, f"update{step}", [latents, grad, got, step_row, pen_row, norm_own, norm_got], [wide_f32, lat_bf16], w_dec)
    return finish(latents, swap(latents, "narrow", far), far)


def solution(mesh):
    return jax.shard_map(
        local,
        mesh=mesh,
        in_specs=(
            P("wide", "narrow"),
            P("wide"),
            P("narrow", "wide"),
            P("wide"),
            P("wide", "narrow"),
            P("narrow"),
            P(),
            P(),
        ),
        out_specs=P(None, "wide"),
        check_vma=False,
    )
```

time: 364 us -> 124 us (0.34)
  waiting for transfers between devices: 215 us -> 36.5 us
  matrix products: 76.4 us -> 0 us
  Pallas kernels: 0 us -> 56 us
  blocking collectives: 43 us -> 0 us
  starting transfers between devices: 0.35 us -> 27.9 us
  other arithmetic: 13.2 us -> 0.01 us
  between operations: 14.5 us -> 1.6 us
    psum x5 -> x0, waiting for transfers between devices: 215 us -> none  [the longest x2 119 us: local(): lax.psum(jnp.dot(code_bf, w_dec, preferred_element_type=jnp.float32), 'wi...]
    dot_general x6 -> x0, matrix products: 76.4 us -> none  [the longest x2 31.6 us: local(): jnp.dot(code_bf, w_dec, preferred_element_type=jnp.float32)]
    pallas_call x0 -> x34, Pallas kernels: none -> 56 us  [local_call(): pl.pallas_call(body, out_shape=outs, in_specs=specs, out_specs=[out_spec]...]
    ppermute x0 -> x22, waiting for transfers between devices: none -> 36.5 us  [swap(): return lax.ppermute(value, axis, pairs)]
    all_gather x1 -> x0, blocking collectives: 32.3 us -> none  [local(): all_pairs = lax.all_gather(own_pairs, 'wide', axis=0, tiled=True)]
    ppermute x0 -> x22, starting transfers between devices: none -> 27.9 us  [swap(): return lax.ppermute(value, axis, pairs)]
    dot_general x1 -> x0, other arithmetic: 11.5 us -> none  [local(): jnp.einsum('ld,ld->l', w_dec, w_dec, preferred_element_type=jnp.float32)]
    psum x1 -> x0, blocking collectives: 10.7 us -> none  [local(): lax.psum((pre_part, square_base, square_inst), 'narrow')]
  transfers between devices with their start and end apart: 5 -> 22, of which waited for: 5 -> 18; matrix products, arithmetic and copies ran while one was open for 3% -> 0% of each run, Pallas kernels for 0% -> 31%
where the time goes in v1:
time: 124 us
  Pallas kernels  56 us (45%)
  waiting for transfers between devices  36.5 us (29%)
  starting transfers between devices  27.9 us (22%)
  local copies, waits for them, and re-layouts  1.62 us (1%)
  between operations  1.6 us (1%)
    pallas_call x34, Pallas kernels, local_call(): pl.pallas_call(body, out_shape=outs, in_specs=specs, out_specs=[out_spec]...  56 us
    ppermute x22, waiting for transfers between devices, swap(): return lax.ppermute(value, axis, pairs)  36.5 us
    ppermute x22, starting transfers between devices, swap(): return lax.ppermute(value, axis, pairs)  27.9 us
  transfers between devices with their start and end apart: 22, of which 18 were waited for; matrix products, arithmetic and copies ran while one was open for 0% of the time, Pallas kernels for 31%

profile of v1, /device:TPU:0, one launch (start us, length us, event | category | flops | bytes accessed | tf_op | source)
XLA Modules:
  0.0 123.6 jit_solution(18238008556585302914)
XLA Ops:
  1.3 0.9 copy-done
  2.9 1.1 select.1
  4.0 3.0 %collective-permute-start = (bf16[2,4096]{1,0:T(2,128)(2,1)S(1)}, bf16[2,4096]{1,0:T(2,128)(2,1)S(1)}, u32[]{:S(2)}, u32[]{:S(2)}) collective-permute-start(bf16[2,4096]{1,0:T(2,128)(2,1)S(1)} %get-tuple-element.21.mine_ref), channel_id=1, source_target_pairs={{0,4},{4,0},{8,12},{12,8},{16,20},{20,16},{24,28},{28,24},{1,5},{5... | collective-permute-start | bytes 49160 | tf_op jit(solution)/shard_map/ppermute | solution.py:19
  7.0 1.7 %collective-permute-done.other_ref = bf16[2,4096]{1,0:T(2,128)(2,1)S(1)} collective-permute-done((bf16[2,4096]{1,0:T(2,128)(2,1)S(1)}, bf16[2,4096]{1,0:T(2,128)(2,1)S(1)}, u32[]{:S(2)}, u32[]{:S(2)}) %collective-permute-start) | collective-permute-done | bytes 16416 | tf_op jit(solution)/shard_map/ppermute | solution.py:19
  8.8 2.2 %collective-permute-start.1 = (bf16[4,4096]{1,0:T(4,128)(2,1)S(1)}, bf16[4,4096]{1,0:T(4,128)(2,1)S(1)}, u32[]{:S(2)}, u32[]{:S(2)}) collective-permute-start(bf16[4,4096]{1,0:T(4,128)(2,1)S(1)} %merge.2.mine_ref), channel_id=1, source_target_pairs={{0,8},{4,12},{8,0},{12,4},{16,24},{20,28},{24,16},{28,20},{1,9},{5... | collective-permute-start | bytes 98312 | tf_op jit(solution)/shard_map/ppermute | solution.py:19
  11.0 1.9 %collective-permute-done.1.other_ref = bf16[4,4096]{1,0:T(4,128)(2,1)S(1)} collective-permute-done((bf16[4,4096]{1,0:T(4,128)(2,1)S(1)}, bf16[4,4096]{1,0:T(4,128)(2,1)S(1)}, u32[]{:S(2)}, u32[]{:S(2)}) %collective-permute-start.1) | collective-permute-done | bytes 32800 | tf_op jit(solution)/shard_map/ppermute | solution.py:19
  12.9 3.1 %collective-permute-start.2 = (bf16[8,4096]{1,0:T(8,128)(2,1)S(1)}, bf16[8,4096]{1,0:T(8,128)(2,1)S(1)}, u32[]{:S(2)}, u32[]{:S(2)}) collective-permute-start(bf16[8,4096]{1,0:T(8,128)(2,1)S(1)} %merge.3.mine_ref), channel_id=1, source_target_pairs={{0,16},{4,20},{8,24},{12,28},{16,0},{20,4},{24,8},{28,12},{1,17},{... | collective-permute-start | bytes 196616 | tf_op jit(solution)/shard_map/ppermute | solution.py:19
  16.1 2.2 %collective-permute-done.2.other_ref = bf16[8,4096]{1,0:T(8,128)(2,1)S(1)} collective-permute-done((bf16[8,4096]{1,0:T(8,128)(2,1)S(1)}, bf16[8,4096]{1,0:T(8,128)(2,1)S(1)}, u32[]{:S(2)}, u32[]{:S(2)}) %collective-permute-start.2) | collective-permute-done | bytes 65568 | tf_op jit(solution)/shard_map/ppermute | solution.py:19
  18.9 6.7 %enc_other.1 = f32[16,2048]{1,0:T(8,128)S(1)} custom-call(bf16[16,4096]{1,0:T(8,128)(2,1)S(1)} %get-tuple-element.24.x_ref, bf16[4096,4096]{1,0:T(8,128)(2,1)} %w_ref.18), custom_call_target="tpu_custom_call" | custom-call | flops 268435456 | bytes 8388608 | tf_op jit(solution)/shard_map/enc_other/pallas_call | solution.py:46
  25.5 1.9 %collective-permute-start.3 = (f32[16,2048]{1,0:T(8,128)S(1)}, f32[16,2048]{1,0:T(8,128)S(1)}, u32[]{:S(2)}, u32[]{:S(2)}) collective-permute-start(f32[16,2048]{1,0:T(8,128)S(1)} %enc_other.1), channel_id=1, source_target_pairs={{0,2},{1,3},{2,0},{3,1},{4,6},{5,7},{6,4},{7,5},{8,10},{9,11},{10,... | collective-permute-start | bytes 393224 | tf_op jit(solution)/shard_map/ppermute | solution.py:19
  27.5 6.6 %enc_own.1.refs_0_ = f32[16,2048]{1,0:T(8,128)S(1)} custom-call(bf16[16,4096]{1,0:T(8,128)(2,1)S(1)} %get-tuple-element.24.x_ref, bf16[4096,4096]{1,0:T(8,128)(2,1)} %w_ref.18), custom_call_target="tpu_custom_call" | custom-call | flops 268435456 | bytes 8388608 | tf_op jit(solution)/shard_map/enc_own/pallas_call | solution.py:46
  34.2 1.3 %collective-permute-done.4.refs_1_ = f32[16,2048]{1,0:T(8,128)S(1)} collective-permute-done((f32[16,2048]{1,0:T(8,128)S(1)}, f32[16,2048]{1,0:T(8,128)S(1)}, u32[]{:S(2)}, u32[]{:S(2)}) %collective-permute-start.4) | collective-permute-done | bytes 131104 | tf_op jit(solution)/shard_map/ppermute | solution.py:19
  35.8 2.6 %rebuild_a0.1.rest_0_ = f32[16,4096]{1,0:T(8,128)S(1)} custom-call(bf16[16,2048]{1,0:T(8,128)(2,1)S(1)} %get-tuple-element.27.x_ref, bf16[4096,4096]{1,0:T(8,128)(2,1)S(1)} %bitcast.7), custom_call_target="tpu_custom_call" | custom-call | flops 268435456 | bytes 8388608 | tf_op jit(solution)/shard_map/rebuild_a0/pallas_call | solution.py:46
  38.5 1.5 %collective-permute-done.5.x_ref = bf16[16,2048]{1,0:T(8,128)(2,1)S(1)} collective-permute-done((bf16[16,2048]{1,0:T(8,128)(2,1)S(1)}, bf16[16,2048]{1,0:T(8,128)(2,1)S(1)}, u32[]{:S(2)}, u32[]{:S(2)}) %collective-permute-start.5) | collective-permute-done | bytes 65568 | tf_op jit(solution)/shard_map/ppermute | solution.py:19
  39.9 1.3 %rebuild_b0.1 = bf16[16,2048]{1,0:T(8,128)(2,1)S(1)} custom-call(bf16[16,2048]{1,0:T(8,128)(2,1)S(1)} %collective-permute-done.5.x_ref, bf16[4096,4096]{1,0:T(8,128)(2,1)S(1)} %bitcast.7, f32[16,4096]{1,0:T(8,128)S(1)} %rebuild_a0.1.rest_0_), custom_call_target="tpu_custom_call" | custom-call | flops 134217728 | bytes 4194304 | tf_op jit(solution)/shard_map/rebuild_b0/pallas_call | solution.py:46
  41.2 1.5 %collective-permute-start.6 = (bf16[16,2048]{1,0:T(8,128)(2,1)S(1)}, bf16[16,2048]{1,0:T(8,128)(2,1)S(1)}, u32[]{:S(2)}, u32[]{:S(2)}) collective-permute-start(bf16[16,2048]{1,0:T(8,128)(2,1)S(1)} %rebuild_b0.1), channel_id=1, source_target_pairs={{0,4},{4,0},{8,12},{12,8},{16,20},{20,16},{24,28},{28,24},{1,5},{5... | collective-permute-start | bytes 196616 | tf_op jit(solution)/shard_map/ppermute | solution.py:19
  42.7 1.3 %rebuild_c0.1.refs_0_ = f32[16,2048]{1,0:T(8,128)S(1)} custom-call(bf16[16,2048]{1,0:T(8,128)(2,1)S(1)} %collective-permute-done.5.x_ref, bf16[4096,4096]{1,0:T(8,128)(2,1)S(1)} %bitcast.7, f32[16,4096]{1,0:T(8,128)S(1)} %rebuild_a0.1.rest_0_), custom_call_target="tpu_custom_call" | custom-call | flops 134217728 | bytes 4194304 | tf_op jit(solution)/shard_map/rebuild_c0/pallas_call | solution.py:46
  44.0 1.5 %collective-permute-done.6.refs_1_ = bf16[16,2048]{1,0:T(8,128)(2,1)S(1)} collective-permute-done((bf16[16,2048]{1,0:T(8,128)(2,1)S(1)}, bf16[16,2048]{1,0:T(8,128)(2,1)S(1)}, u32[]{:S(2)}, u32[]{:S(2)}) %collective-permute-start.6) | collective-permute-done | bytes 65568 | tf_op jit(solution)/shard_map/ppermute | solution.py:19
  45.5 1.6 %collective-permute-start.7 = (bf16[16,2048]{1,0:T(8,128)(2,1)S(1)}, bf16[16,2048]{1,0:T(8,128)(2,1)S(1)}, u32[]{:S(2)}, u32[]{:S(2)}) collective-permute-start(bf16[16,2048]{1,0:T(8,128)(2,1)S(1)} %rebuilt0.2.refs_0_), channel_id=1, source_target_pairs={{0,8},{4,12},{8,0},{12,4},{16,24},{20,28},{24,16},{28,20},{1,9},{5... | collective-permute-start | bytes 196616 | tf_op jit(solution)/shard_map/ppermute | solution.py:19
  47.2 2.7 %collective-permute-done.7.refs_1_ = bf16[16,2048]{1,0:T(8,128)(2,1)S(1)} collective-permute-done((bf16[16,2048]{1,0:T(8,128)(2,1)S(1)}, bf16[16,2048]{1,0:T(8,128)(2,1)S(1)}, u32[]{:S(2)}, u32[]{:S(2)}) %collective-permute-start.7) | collective-permute-done | bytes 65568 | tf_op jit(solution)/shard_map/ppermute | solution.py:19
  49.9 3.1 %collective-permute-start.8 = (bf16[16,2048]{1,0:T(8,128)(2,1)S(1)}, bf16[16,2048]{1,0:T(8,128)(2,1)S(1)}, u32[]{:S(2)}, u32[]{:S(2)}) collective-permute-start(bf16[16,2048]{1,0:T(8,128)(2,1)S(1)} %rebuilt0.3.refs_0_), channel_id=1, source_target_pairs={{0,16},{4,20},{8,24},{12,28},{16,0},{20,4},{24,8},{28,12},{1,17},{... | collective-permute-start | bytes 196616 | tf_op jit(solution)/shard_map/ppermute | solution.py:19
  53.0 2.2 %collective-permute-done.8.refs_1_ = bf16[16,2048]{1,0:T(8,128)(2,1)S(1)} collective-permute-done((bf16[16,2048]{1,0:T(8,128)(2,1)S(1)}, bf16[16,2048]{1,0:T(8,128)(2,1)S(1)}, u32[]{:S(2)}, u32[]{:S(2)}) %collective-permute-start.8) | collective-permute-done | bytes 65568 | tf_op jit(solution)/shard_map/ppermute | solution.py:19
  55.3 1.6 %collective-permute-start.9 = (bf16[16,2048]{1,0:T(8,128)(2,1)S(1)}, bf16[16,2048]{1,0:T(8,128)(2,1)S(1)}, u32[]{:S(2)}, u32[]{:S(2)}) collective-permute-start(bf16[16,2048]{1,0:T(8,128)(2,1)S(1)} %residual0.1.x_ref), channel_id=1, source_target_pairs={{0,4},{4,0},{8,12},{12,8},{16,20},{20,16},{24,28},{28,24},{1,5},{5... | collective-permute-start | bytes 196616 | tf_op jit(solution)/shard_map/ppermute | solution.py:19
  56.9 4.8 %grad_a0.1.rest_0_ = f32[16,4096]{1,0:T(8,128)S(1)} custom-call(bf16[16,2048]{1,0:T(8,128)(2,1)S(1)} %residual0.1.x_ref, bf16[4096,4096]{1,0:T(8,128)(2,1)S(1)} %bitcast.7), custom_call_target="tpu_custom_call" | custom-call | flops 268435456 | bytes 8388608 | tf_op jit(solution)/shard_map/grad_a0/pallas_call | solution.py:46
  61.6 2.4 %grad_b0.1 = bf16[16,2048]{1,0:T(8,128)(2,1)S(1)} custom-call(bf16[16,2048]{1,0:T(8,128)(2,1)S(1)} %collective-permute-done.9.x_ref, bf16[4096,4096]{1,0:T(8,128)(2,1)S(1)} %bitcast.7, f32[16,4096]{1,0:T(8,128)S(1)} %grad_a0.1.rest_0_), custom_call_target="tpu_custom_call" | custom-call | flops 134217728 | bytes 4194304 | tf_op jit(solution)/shard_map/grad_b0/pallas_call | solution.py:46
  64.4 2.4 %grad_c0.1.refs_0_ = f32[16,2048]{1,0:T(8,128)S(1)} custom-call(bf16[16,2048]{1,0:T(8,128)(2,1)S(1)} %collective-permute-done.9.x_ref, bf16[4096,4096]{1,0:T(8,128)(2,1)S(1)} %bitcast.7, f32[16,4096]{1,0:T(8,128)S(1)} %grad_a0.1.rest_0_), custom_call_target="tpu_custom_call" | custom-call | flops 134217728 | bytes 4194304 | tf_op jit(solution)/shard_map/grad_c0/pallas_call | solution.py:46
  66.8 1.5 %collective-permute-done.10.refs_1_ = bf16[16,2048]{1,0:T(8,128)(2,1)S(1)} collective-permute-done((bf16[16,2048]{1,0:T(8,128)(2,1)S(1)}, bf16[16,2048]{1,0:T(8,128)(2,1)S(1)}, u32[]{:S(2)}, u32[]{:S(2)}) %collective-permute-start.10) | collective-permute-done | bytes 65568 | tf_op jit(solution)/shard_map/ppermute | solution.py:19
  68.4 9.7 %squares.1.refs_0_ = f32[2,2048]{1,0:T(2,128)S(1)} custom-call(bf16[4096,4096]{1,0:T(8,128)(2,1)S(1)} %bitcast.7), custom_call_target="tpu_custom_call" | custom-call | flops 536870912 | bytes 16777216 | tf_op jit(solution)/shard_map/squares/pallas_call | solution.py:46
  78.7 0.8 collective-permute-done.12.refs_1_
  80.0 3.3 %collective-permute-done.13.refs_6_ = f32[1,2048]{1,0:T(1,128)S(1)} collective-permute-done((f32[1,2048]{1,0:T(1,128)S(1)}, f32[1,2048]{1,0:T(1,128)S(1)}, u32[]{:S(2)}, u32[]{:S(2)}) %collective-permute-start.13) | collective-permute-done | bytes 8224 | tf_op jit(solution)/shard_map/ppermute | solution.py:19
  83.7 2.6 %rebuild_a1.1.rest_0_ = f32[16,4096]{1,0:T(8,128)S(1)} custom-call(bf16[16,2048]{1,0:T(8,128)(2,1)S(1)} %get-tuple-element.35.x_ref, bf16[4096,4096]{1,0:T(8,128)(2,1)S(1)} %bitcast.7), custom_call_target="tpu_custom_call" | custom-call | flops 268435456 | bytes 8388608 | tf_op jit(solution)/shard_map/rebuild_a1/pallas_call | solution.py:46
  86.4 1.3 %collective-permute-done.14.x_ref = bf16[16,2048]{1,0:T(8,128)(2,1)S(1)} collective-permute-done((bf16[16,2048]{1,0:T(8,128)(2,1)S(1)}, bf16[16,2048]{1,0:T(8,128)(2,1)S(1)}, u32[]{:S(2)}, u32[]{:S(2)}) %collective-permute-start.14) | collective-permute-done | bytes 65568 | tf_op jit(solution)/shard_map/ppermute | solution.py:19
  87.6 1.3 %rebuild_b1.1 = bf16[16,2048]{1,0:T(8,128)(2,1)S(1)} custom-call(bf16[16,2048]{1,0:T(8,128)(2,1)S(1)} %collective-permute-done.14.x_ref, bf16[4096,4096]{1,0:T(8,128)(2,1)S(1)} %bitcast.7, f32[16,4096]{1,0:T(8,128)S(1)} %rebuild_a1.1.rest_0_), custom_call_target="tpu_custom_call" | custom-call | flops 134217728 | bytes 4194304 | tf_op jit(solution)/shard_map/rebuild_b1/pallas_call | solution.py:46
  89.5 1.3 %rebuild_c1.1.refs_0_ = f32[16,2048]{1,0:T(8,128)S(1)} custom-call(bf16[16,2048]{1,0:T(8,128)(2,1)S(1)} %collective-permute-done.14.x_ref, bf16[4096,4096]{1,0:T(8,128)(2,1)S(1)} %bitcast.7, f32[16,4096]{1,0:T(8,128)S(1)} %rebuild_a1.1.rest_0_), custom_call_target="tpu_custom_call" | custom-call | flops 134217728 | bytes 4194304 | tf_op jit(solution)/shard_map/rebuild_c1/pallas_call | solution.py:46
  90.8 2.4 %collective-permute-done.15.refs_1_ = bf16[16,2048]{1,0:T(8,128)(2,1)S(1)} collective-permute-done((bf16[16,2048]{1,0:T(8,128)(2,1)S(1)}, bf16[16,2048]{1,0:T(8,128)(2,1)S(1)}, u32[]{:S(2)}, u32[]{:S(2)}) %collective-permute-start.15) | collective-permute-done | bytes 65568 | tf_op jit(solution)/shard_map/ppermute | solution.py:19
  93.3 1.8 %collective-permute-start.16 = (bf16[16,2048]{1,0:T(8,128)(2,1)S(1)}, bf16[16,2048]{1,0:T(8,128)(2,1)S(1)}, u32[]{:S(2)}, u32[]{:S(2)}) collective-permute-start(bf16[16,2048]{1,0:T(8,128)(2,1)S(1)} %rebuilt1.2.refs_0_), channel_id=1, source_target_pairs={{0,8},{4,12},{8,0},{12,4},{16,24},{20,28},{24,16},{28,20},{1,9},{5... | collective-permute-start | bytes 196616 | tf_op jit(solution)/shard_map/ppermute | solution.py:19
  95.0 2.6 %collective-permute-done.16.refs_1_ = bf16[16,2048]{1,0:T(8,128)(2,1)S(1)} collective-permute-done((bf16[16,2048]{1,0:T(8,128)(2,1)S(1)}, bf16[16,2048]{1,0:T(8,128)(2,1)S(1)}, u32[]{:S(2)}, u32[]{:S(2)}) %collective-permute-start.16) | collective-permute-done | bytes 65568 | tf_op jit(solution)/shard_map/ppermute | solution.py:19
  97.6 3.3 %collective-permute-start.17 = (bf16[16,2048]{1,0:T(8,128)(2,1)S(1)}, bf16[16,2048]{1,0:T(8,128)(2,1)S(1)}, u32[]{:S(2)}, u32[]{:S(2)}) collective-permute-start(bf16[16,2048]{1,0:T(8,128)(2,1)S(1)} %rebuilt1.3.refs_0_), channel_id=1, source_target_pairs={{0,16},{4,20},{8,24},{12,28},{16,0},{20,4},{24,8},{28,12},{1,17},{... | collective-permute-start | bytes 196616 | tf_op jit(solution)/shard_map/ppermute | solution.py:19
  100.9 2.2 %collective-permute-done.17.refs_1_ = bf16[16,2048]{1,0:T(8,128)(2,1)S(1)} collective-permute-done((bf16[16,2048]{1,0:T(8,128)(2,1)S(1)}, bf16[16,2048]{1,0:T(8,128)(2,1)S(1)}, u32[]{:S(2)}, u32[]{:S(2)}) %collective-permute-start.17) | collective-permute-done | bytes 65568 | tf_op jit(solution)/shard_map/ppermute | solution.py:19
  103.8 4.8 %grad_a1.1.rest_0_ = f32[16,4096]{1,0:T(8,128)S(1)} custom-call(bf16[16,2048]{1,0:T(8,128)(2,1)S(1)} %residual1.1.x_ref, bf16[4096,4096]{1,0:T(8,128)(2,1)S(1)} %bitcast.7), custom_call_target="tpu_custom_call" | custom-call | flops 268435456 | bytes 8388608 | tf_op jit(solution)/shard_map/grad_a1/pallas_call | solution.py:46
  108.5 2.4 %grad_b1.1 = bf16[16,2048]{1,0:T(8,128)(2,1)S(1)} custom-call(bf16[16,2048]{1,0:T(8,128)(2,1)S(1)} %collective-permute-done.18.x_ref, bf16[4096,4096]{1,0:T(8,128)(2,1)S(1)} %bitcast.7, f32[16,4096]{1,0:T(8,128)S(1)} %grad_a1.1.rest_0_), custom_call_target="tpu_custom_call" | custom-call | flops 134217728 | bytes 4194304 | tf_op jit(solution)/shard_map/grad_b1/pallas_call | solution.py:46
  111.0 0.7 collective-permute-start.19
  111.7 2.4 %grad_c1.1.refs_0_ = f32[16,2048]{1,0:T(8,128)S(1)} custom-call(bf16[16,2048]{1,0:T(8,128)(2,1)S(1)} %collective-permute-done.18.x_ref, bf16[4096,4096]{1,0:T(8,128)(2,1)S(1)} %bitcast.7, f32[16,4096]{1,0:T(8,128)S(1)} %grad_a1.1.rest_0_), custom_call_target="tpu_custom_call" | custom-call | flops 134217728 | bytes 4194304 | tf_op jit(solution)/shard_map/grad_c1/pallas_call | solution.py:46
  114.1 1.2 collective-permute-done.19.refs_1_
  115.3 1.3 %collective-permute-done.20.refs_2_ = f32[16,2048]{1,0:T(8,128)S(1)} collective-permute-done((f32[16,2048]{1,0:T(8,128)S(1)}, f32[16,2048]{1,0:T(8,128)S(1)}, u32[]{:S(2)}, u32[]{:S(2)}) %collective-permute-start.20) | collective-permute-done | bytes 131104 | tf_op jit(solution)/shard_map/ppermute | solution.py:19
  117.3 0.7 collective-permute-start.21
  118.0 4.8 %collective-permute-done.21.other_ref = f32[16,2048]{1,0:T(8,128)S(1)} collective-permute-done((f32[16,2048]{1,0:T(8,128)S(1)}, f32[16,2048]{1,0:T(8,128)S(1)}, u32[]{:S(2)}, u32[]{:S(2)}) %collective-permute-start.21) | collective-permute-done | bytes 131104 | tf_op jit(solution)/shard_map/ppermute | solution.py:19
  122.9 0.7 finish.1
  (59 shorter events, 5.7 us)
Async XLA Ops:
  1.3 0.9 copy-start
  2.2 0.7 copy-start.5
  3.9 9.0 %copy-start.1 = (f32[1,2048]{1,0:T(1,128)}, f32[1,2048]{1,0:T(1,128)S(1)}, u32[]{:S(2)}) copy-start(f32[1,2048]{1,0:T(1,128)S(1)} %get-tuple-element.23.after_ref.pen_ref) | copy-start | bytes 24580
  3.9 12.1 %slice-start = ((s8[33554432]{0:T(1024)(128)(4,1)}), s8[4194304]{0:T(1024)(128)(4,1)S(1)}, s32[]{:S(2)}) async-start(s8[33554432]{0:T(1024)(128)(4,1)} %bitcast.6), calls=%async_computation | async-start | bytes 8388608
  3.9 12.1 %slice-start.1 = ((s8[33554432]{0:T(1024)(128)(4,1)}), s8[4194304]{0:T(1024)(128)(4,1)S(1)}, s32[]{:S(2)}) async-start(s8[33554432]{0:T(1024)(128)(4,1)} %bitcast.6), calls=%async_computation.1 | async-start | bytes 8388608
  3.9 12.1 %slice-start.2 = ((s8[33554432]{0:T(1024)(128)(4,1)}), s8[4194304]{0:T(1024)(128)(4,1)S(1)}, s32[]{:S(2)}) async-start(s8[33554432]{0:T(1024)(128)(4,1)} %bitcast.6), calls=%async_computation.2 | async-start | bytes 8388608
  4.0 12.1 %slice-start.3 = ((s8[33554432]{0:T(1024)(128)(4,1)}), s8[4194304]{0:T(1024)(128)(4,1)S(1)}, s32[]{:S(2)}) async-start(s8[33554432]{0:T(1024)(128)(4,1)} %bitcast.6), calls=%async_computation.3 | async-start | bytes 8388608
  4.0 4.8 %collective-permute-start = (bf16[2,4096]{1,0:T(2,128)(2,1)S(1)}, bf16[2,4096]{1,0:T(2,128)(2,1)S(1)}, u32[]{:S(2)}, u32[]{:S(2)}) collective-permute-start(bf16[2,4096]{1,0:T(2,128)(2,1)S(1)} %get-tuple-element.21.mine_ref), channel_id=1, source_target_pairs={{0,4},{4,0},{8,12},{12,8},{16,20},{20,16},{24,28},{28,24},{1,5},{5... | collective-permute-start | bytes 49160 | tf_op jit(solution)/shard_map/ppermute | solution.py:19
  8.8 7.3 %slice-start.4 = ((s8[33554432]{0:T(1024)(128)(4,1)}), s8[4194304]{0:T(1024)(128)(4,1)S(1)}, s32[]{:S(2)}) async-start(s8[33554432]{0:T(1024)(128)(4,1)} %bitcast.6), calls=%async_computation.4 | async-start | bytes 8388608
  8.8 7.3 %slice-start.5 = ((s8[33554432]{0:T(1024)(128)(4,1)}), s8[4194304]{0:T(1024)(128)(4,1)S(1)}, s32[]{:S(2)}) async-start(s8[33554432]{0:T(1024)(128)(4,1)} %bitcast.6), calls=%async_computation.5 | async-start | bytes 8388608
  8.8 7.3 %slice-start.6 = ((s8[33554432]{0:T(1024)(128)(4,1)}), s8[4194304]{0:T(1024)(128)(4,1)S(1)}, s32[]{:S(2)}) async-start(s8[33554432]{0:T(1024)(128)(4,1)} %bitcast.6), calls=%async_computation.6 | async-start | bytes 8388608
  8.8 7.3 %slice-start.7 = ((s8[33554432]{0:T(1024)(128)(4,1)}), s8[4194304]{0:T(1024)(128)(4,1)S(1)}, s32[]{:S(2)}) async-start(s8[33554432]{0:T(1024)(128)(4,1)} %bitcast.6), calls=%async_computation.7 | async-start | bytes 8388608
  8.8 9.5 %copy-start.3 = (f32[4096]{0:T(1024)S(1)}, f32[4096]{0:T(1024)}, u32[]{:S(2)}) copy-start(f32[4096]{0:T(1024)} %param.11) | copy-start | bytes 49156
  8.8 9.5 %copy-start.4 = (f32[4096]{0:T(1024)S(1)}, f32[4096]{0:T(1024)}, u32[]{:S(2)}) copy-start(f32[4096]{0:T(1024)} %param.13) | copy-start | bytes 49156
  8.8 4.1 %collective-permute-start.1 = (bf16[4,4096]{1,0:T(4,128)(2,1)S(1)}, bf16[4,4096]{1,0:T(4,128)(2,1)S(1)}, u32[]{:S(2)}, u32[]{:S(2)}) collective-permute-start(bf16[4,4096]{1,0:T(4,128)(2,1)S(1)} %merge.2.mine_ref), channel_id=1, source_target_pairs={{0,8},{4,12},{8,0},{12,4},{16,24},{20,28},{24,16},{28,20},{1,9},{5... | collective-permute-start | bytes 98312 | tf_op jit(solution)/shard_map/ppermute | solution.py:19
  12.9 5.3 %collective-permute-start.2 = (bf16[8,4096]{1,0:T(8,128)(2,1)S(1)}, bf16[8,4096]{1,0:T(8,128)(2,1)S(1)}, u32[]{:S(2)}, u32[]{:S(2)}) collective-permute-start(bf16[8,4096]{1,0:T(8,128)(2,1)S(1)} %merge.3.mine_ref), channel_id=1, source_target_pairs={{0,16},{4,20},{8,24},{12,28},{16,0},{20,4},{24,8},{28,12},{1,17},{... | collective-permute-start | bytes 196616 | tf_op jit(solution)/shard_map/ppermute | solution.py:19
  16.0 2.3 %copy-start.2 = (f32[1,2048]{1,0:T(1,128)S(1)}, f32[1,2048]{1,0:T(1,128)}, u32[]{:S(2)}) copy-start(f32[1,2048]{1,0:T(1,128)} %copy-done.1) | copy-start | bytes 24580
  25.5 8.6 %collective-permute-start.3 = (f32[16,2048]{1,0:T(8,128)S(1)}, f32[16,2048]{1,0:T(8,128)S(1)}, u32[]{:S(2)}, u32[]{:S(2)}) collective-permute-start(f32[16,2048]{1,0:T(8,128)S(1)} %enc_other.1), channel_id=1, source_target_pairs={{0,2},{1,3},{2,0},{3,1},{4,6},{5,7},{6,4},{7,5},{8,10},{9,11},{10,... | collective-permute-start | bytes 393224 | tf_op jit(solution)/shard_map/ppermute | solution.py:19
  34.1 1.4 %collective-permute-start.4 = (f32[16,2048]{1,0:T(8,128)S(1)}, f32[16,2048]{1,0:T(8,128)S(1)}, u32[]{:S(2)}, u32[]{:S(2)}) collective-permute-start(f32[16,2048]{1,0:T(8,128)S(1)} %pre.1.refs_0_), channel_id=1, source_target_pairs={{0,1},{1,0},{2,3},{3,2},{4,5},{5,4},{6,7},{7,6},{8,9},{9,8},{10,11... | collective-permute-start | bytes 393224 | tf_op jit(solution)/shard_map/ppermute | solution.py:19
  35.6 4.3 %collective-permute-start.5 = (bf16[16,2048]{1,0:T(8,128)(2,1)S(1)}, bf16[16,2048]{1,0:T(8,128)(2,1)S(1)}, u32[]{:S(2)}, u32[]{:S(2)}) collective-permute-start(bf16[16,2048]{1,0:T(8,128)(2,1)S(1)} %get-tuple-element.27.x_ref), channel_id=1, source_target_pairs={{0,2},{1,3},{2,0},{3,1},{4,6},{5,7},{6,4},{7,5},{8,10},{9,11},{10,... | collective-permute-start | bytes 196616 | tf_op jit(solution)/shard_map/ppermute | solution.py:19
  41.2 4.3 %collective-permute-start.6 = (bf16[16,2048]{1,0:T(8,128)(2,1)S(1)}, bf16[16,2048]{1,0:T(8,128)(2,1)S(1)}, u32[]{:S(2)}, u32[]{:S(2)}) collective-permute-start(bf16[16,2048]{1,0:T(8,128)(2,1)S(1)} %rebuild_b0.1), channel_id=1, source_target_pairs={{0,4},{4,0},{8,12},{12,8},{16,20},{20,16},{24,28},{28,24},{1,5},{5... | collective-permute-start | bytes 196616 | tf_op jit(solution)/shard_map/ppermute | solution.py:19
  45.5 4.3 %collective-permute-start.7 = (bf16[16,2048]{1,0:T(8,128)(2,1)S(1)}, bf16[16,2048]{1,0:T(8,128)(2,1)S(1)}, u32[]{:S(2)}, u32[]{:S(2)}) collective-permute-start(bf16[16,2048]{1,0:T(8,128)(2,1)S(1)} %rebuilt0.2.refs_0_), channel_id=1, source_target_pairs={{0,8},{4,12},{8,0},{12,4},{16,24},{20,28},{24,16},{28,20},{1,9},{5... | collective-permute-start | bytes 196616 | tf_op jit(solution)/shard_map/ppermute | solution.py:19
  49.9 5.4 %collective-permute-start.8 = (bf16[16,2048]{1,0:T(8,128)(2,1)S(1)}, bf16[16,2048]{1,0:T(8,128)(2,1)S(1)}, u32[]{:S(2)}, u32[]{:S(2)}) collective-permute-start(bf16[16,2048]{1,0:T(8,128)(2,1)S(1)} %rebuilt0.3.refs_0_), channel_id=1, source_target_pairs={{0,16},{4,20},{8,24},{12,28},{16,0},{20,4},{24,8},{28,12},{1,17},{... | collective-permute-start | bytes 196616 | tf_op jit(solution)/shard_map/ppermute | solution.py:19
  55.3 6.3 %collective-permute-start.9 = (bf16[16,2048]{1,0:T(8,128)(2,1)S(1)}, bf16[16,2048]{1,0:T(8,128)(2,1)S(1)}, u32[]{:S(2)}, u32[]{:S(2)}) collective-permute-start(bf16[16,2048]{1,0:T(8,128)(2,1)S(1)} %residual0.1.x_ref), channel_id=1, source_target_pairs={{0,4},{4,0},{8,12},{12,8},{16,20},{20,16},{24,28},{28,24},{1,5},{5... | collective-permute-start | bytes 196616 | tf_op jit(solution)/shard_map/ppermute | solution.py:19
  64.0 4.3 %collective-permute-start.10 = (bf16[16,2048]{1,0:T(8,128)(2,1)S(1)}, bf16[16,2048]{1,0:T(8,128)(2,1)S(1)}, u32[]{:S(2)}, u32[]{:S(2)}) collective-permute-start(bf16[16,2048]{1,0:T(8,128)(2,1)S(1)} %grad_b0.1), channel_id=1, source_target_pairs={{0,2},{1,3},{2,0},{3,1},{4,6},{5,7},{6,4},{7,5},{8,10},{9,11},{10,... | collective-permute-start | bytes 196616 | tf_op jit(solution)/shard_map/ppermute | solution.py:19
  68.3 14.9 %collective-permute-start.11 = (f32[16,2048]{1,0:T(8,128)S(1)}, f32[16,2048]{1,0:T(8,128)S(1)}, u32[]{:S(2)}, u32[]{:S(2)}) collective-permute-start(f32[16,2048]{1,0:T(8,128)S(1)} %grad0.1.refs_1_), channel_id=1, source_target_pairs={{0,1},{1,0},{2,3},{3,2},{4,5},{5,4},{6,7},{7,6},{8,9},{9,8},{10,11... | collective-permute-start | bytes 393224 | tf_op jit(solution)/shard_map/ppermute | solution.py:19
  78.2 1.4 %collective-permute-start.12 = (f32[2,2048]{1,0:T(2,128)S(1)}, f32[2,2048]{1,0:T(2,128)S(1)}, u32[]{:S(2)}, u32[]{:S(2)}) collective-permute-start(f32[2,2048]{1,0:T(2,128)S(1)} %squares.1.refs_0_), channel_id=1, source_target_pairs={{0,1},{1,0},{2,3},{3,2},{4,5},{5,4},{6,7},{7,6},{8,9},{9,8},{10,11... | collective-permute-start | bytes 49160 | tf_op jit(solution)/shard_map/ppermute | solution.py:19
  79.6 3.7 %collective-permute-start.13 = (f32[1,2048]{1,0:T(1,128)S(1)}, f32[1,2048]{1,0:T(1,128)S(1)}, u32[]{:S(2)}, u32[]{:S(2)}) collective-permute-start(f32[1,2048]{1,0:T(1,128)S(1)} %get-tuple-element.33), channel_id=1, source_target_pairs={{0,2},{1,3},{2,0},{3,1},{4,6},{5,7},{6,4},{7,5},{8,10},{9,11},{10,... | collective-permute-start | bytes 24584 | tf_op jit(solution)/shard_map/ppermute | solution.py:19
  83.3 4.3 %collective-permute-start.14 = (bf16[16,2048]{1,0:T(8,128)(2,1)S(1)}, bf16[16,2048]{1,0:T(8,128)(2,1)S(1)}, u32[]{:S(2)}, u32[]{:S(2)}) collective-permute-start(bf16[16,2048]{1,0:T(8,128)(2,1)S(1)} %get-tuple-element.35.x_ref), channel_id=1, source_target_pairs={{0,2},{1,3},{2,0},{3,1},{4,6},{5,7},{6,4},{7,5},{8,10},{9,11},{10,... | collective-permute-start | bytes 196616 | tf_op jit(solution)/shard_map/ppermute | solution.py:19
  89.0 4.3 %collective-permute-start.15 = (bf16[16,2048]{1,0:T(8,128)(2,1)S(1)}, bf16[16,2048]{1,0:T(8,128)(2,1)S(1)}, u32[]{:S(2)}, u32[]{:S(2)}) collective-permute-start(bf16[16,2048]{1,0:T(8,128)(2,1)S(1)} %rebuild_b1.1), channel_id=1, source_target_pairs={{0,4},{4,0},{8,12},{12,8},{16,20},{20,16},{24,28},{28,24},{1,5},{5... | collective-permute-start | bytes 196616 | tf_op jit(solution)/shard_map/ppermute | solution.py:19
  93.3 4.3 %collective-permute-start.16 = (bf16[16,2048]{1,0:T(8,128)(2,1)S(1)}, bf16[16,2048]{1,0:T(8,128)(2,1)S(1)}, u32[]{:S(2)}, u32[]{:S(2)}) collective-permute-start(bf16[16,2048]{1,0:T(8,128)(2,1)S(1)} %rebuilt1.2.refs_0_), channel_id=1, source_target_pairs={{0,8},{4,12},{8,0},{12,4},{16,24},{20,28},{24,16},{28,20},{1,9},{5... | collective-permute-start | bytes 196616 | tf_op jit(solution)/shard_map/ppermute | solution.py:19
  97.6 5.5 %collective-permute-start.17 = (bf16[16,2048]{1,0:T(8,128)(2,1)S(1)}, bf16[16,2048]{1,0:T(8,128)(2,1)S(1)}, u32[]{:S(2)}, u32[]{:S(2)}) collective-permute-start(bf16[16,2048]{1,0:T(8,128)(2,1)S(1)} %rebuilt1.3.refs_0_), channel_id=1, source_target_pairs={{0,16},{4,20},{8,24},{12,28},{16,0},{20,4},{24,8},{28,12},{1,17},{... | collective-permute-start | bytes 196616 | tf_op jit(solution)/shard_map/ppermute | solution.py:19
  103.2 5.4 %collective-permute-start.18 = (bf16[16,2048]{1,0:T(8,128)(2,1)S(1)}, bf16[16,2048]{1,0:T(8,128)(2,1)S(1)}, u32[]{:S(2)}, u32[]{:S(2)}) collective-permute-start(bf16[16,2048]{1,0:T(8,128)(2,1)S(1)} %residual1.1.x_ref), channel_id=1, source_target_pairs={{0,4},{4,0},{8,12},{12,8},{16,20},{20,16},{24,28},{28,24},{1,5},{5... | collective-permute-start | bytes 196616 | tf_op jit(solution)/shard_map/ppermute | solution.py:19
  111.0 4.3 %collective-permute-start.19 = (bf16[16,2048]{1,0:T(8,128)(2,1)S(1)}, bf16[16,2048]{1,0:T(8,128)(2,1)S(1)}, u32[]{:S(2)}, u32[]{:S(2)}) collective-permute-start(bf16[16,2048]{1,0:T(8,128)(2,1)S(1)} %grad_b1.1), channel_id=1, source_target_pairs={{0,2},{1,3},{2,0},{3,1},{4,6},{5,7},{6,4},{7,5},{8,10},{9,11},{10,... | collective-permute-start | bytes 196616 | tf_op jit(solution)/shard_map/ppermute | solution.py:19
  115.2 1.4 %collective-permute-start.20 = (f32[16,2048]{1,0:T(8,128)S(1)}, f32[16,2048]{1,0:T(8,128)S(1)}, u32[]{:S(2)}, u32[]{:S(2)}) collective-permute-start(f32[16,2048]{1,0:T(8,128)S(1)} %grad1.1.refs_1_), channel_id=1, source_target_pairs={{0,1},{1,0},{2,3},{3,2},{4,5},{5,4},{6,7},{7,6},{8,9},{9,8},{10,11... | collective-permute-start | bytes 393224 | tf_op jit(solution)/shard_map/ppermute | solution.py:19
  117.3 5.5 %collective-permute-start.21 = (f32[16,2048]{1,0:T(8,128)S(1)}, f32[16,2048]{1,0:T(8,128)S(1)}, u32[]{:S(2)}, u32[]{:S(2)}) collective-permute-start(f32[16,2048]{1,0:T(8,128)S(1)} %get-tuple-element.36.own_ref), channel_id=1, source_target_pairs={{0,2},{1,3},{2,0},{3,1},{4,6},{5,7},{6,4},{7,5},{8,10},{9,11},{10,... | collective-permute-start | bytes 393224 | tf_op jit(solution)/shard_map/ppermute | solution.py:19

commit v2 on v1

--- a/solution.py
+++ b/solution.py
@@ -154,14 +154,16 @@
     return local_call(body, name, [*arrays, w_dec], outs, 1 << 16)
 
 
-def encode(x, w, far, other, name):
+def encode(x, w, w_dec, far, other, name):
     depth, lat = w.shape
     half = lat // 2
-    chunk = tile_of(depth, 512)
+    chunk = tile_of(depth, 256)
     steps = depth // chunk
-    slots = min(4, steps)
-
-    def body(x_ref, w_ref, o_ref, held, sems):
+    slots = min(8, steps)
+    block = tile_of(half, 128)
+    blocks = half // block
+
+    def body(x_ref, w_ref, dec_ref, o_ref, sq_ref, held, sems):
         start = half_start("narrow", far, half, other)
 
         def fetch(k):
@@ -173,25 +175,25 @@
             fetch(k).start()
         for k in range(steps):
             fetch(k).wait()
-            width = tile_of(half, 1024)
-
-            @pl.loop(0, half // width)
-            def _(j):
-                here = pl.ds(pl.multiple_of(j * width, width), width)
-                part = jnp.dot(x_ref[:, k * chunk:(k + 1) * chunk], held[k % slots, :, here], preferred_element_type=F32)
-                if k:
-                    part = part + o_ref[:, here]
-                o_ref[:, here] = part
-
+            part = jnp.dot(x_ref[:, k * chunk:(k + 1) * chunk], held[k % slots], preferred_element_type=F32)
+            o_ref[...] = part + o_ref[...] if k else part
+            for b in range(blocks):
+                if b * steps // blocks == k:
+                    there = pl.ds(pl.multiple_of(start + b * block, block), block)
+                    total = jnp.zeros((block, 128), F32)
+                    for c in range(dec_ref.shape[1] // 128):
+                        value = dec_ref[there, c * 128:(c + 1) * 128].astype(F32)
+                        total = total + value * value
+                    sq_ref[:, b * block:(b + 1) * block] = jnp.sum(total.T, axis=0, keepdims=True)
             if k + slots < steps:
                 fetch(k + slots).start()
 
-    out = jax.ShapeDtypeStruct((x.shape[0], half), F32)
+    outs = [jax.ShapeDtypeStruct((x.shape[0], half), F32), jax.ShapeDtypeStruct((1, half), F32)]
     scratch = [pltpu.VMEM((slots, chunk, half), BF16), pltpu.SemaphoreType.DMA((slots,))]
-    return local_call(body, name, [x, w], out, 2 * x.shape[0] * depth * half, scratch=scratch, vmem=12, in_hbm=(1,))
-
-
-def product(x, w, acc, dtype, depth_at, width_at, transposed, name):
+    return local_call(body, name, [x, w, w_dec], outs, 2 * x.shape[0] * depth * half, scratch=scratch, in_hbm=(1,))
+
+
+def product(x, w, acc, dtype, depth_at, width_at, transposed, name, after=()):
     depth = x.shape[1]
     width = w.shape[0 if transposed else 1]
     if width_at is not None:
@@ -199,7 +201,7 @@
     step = tile_of(width, 1024)
 
     def body(x_ref, w_ref, *rest):
-        *acc_ref, o_ref = rest
+        acc_ref, o_ref = rest[:0 if acc is None else 1], rest[-1]
         deep = pl.ds(half_start(*depth_at[:2], depth, depth_at[2]), depth)
         base = 0 if width_at is None else half_start(*width_at[:2], width, width_at[2])
 
@@ -216,31 +218,8 @@
             o_ref[:, here] = part.astype(dtype)
 
     out = jax.ShapeDtypeStruct((x.shape[0], width), dtype)
-    arrays = [x, w] + ([] if acc is None else [acc])
+    arrays = [x, w] + ([] if acc is None else [acc]) + list(after)
     return local_call(body, name, arrays, out, 2 * x.shape[0] * depth * width)
-
-
-def squares_of(w, far):
-    rows, cols = w.shape
-    half = rows // 2
-    step = tile_of(half, 128)
-
-    def body(w_ref, o_ref):
-        for other in (False, True):
-            start = half_start("narrow", far, half, other)
-
-            @pl.loop(0, half // step)
-            def _(j):
-                here = pl.multiple_of(j * step, step)
-                there = pl.ds(pl.multiple_of(start + here, step), step)
-                total = jnp.zeros((step, 128), F32)
-                for c in range(cols // 128):
-                    part = w_ref[there, c * 128:(c + 1) * 128].astype(F32)
-                    total = total + part * part
-                o_ref[int(other):int(other) + 1, pl.ds(here, step)] = jnp.sum(total.T, axis=0, keepdims=True)
-
-    out = jax.ShapeDtypeStruct((2, half), F32)
-    return local_call(body, "squares", [w], out, 2 * 16 * rows * cols)
 
 
 def finish(own, other, far):
@@ -282,21 +261,17 @@
             (value,) = pointwise(lambda a, b: (a + b,), name, [value, swap(value, "narrow", bit)], [jax.ShapeDtypeStruct(value.shape, F32)], w_dec)
         return value
 
-    got = swap(encode(pairs, w_enc, far, True, "enc_other"), "narrow", far)
-    (pre,) = pointwise(lambda a, b: (a + b,), "pre", [encode(pairs, w_enc, far, False, "enc_own"), got], [wide_f32], w_dec)
+    send, squares_other = encode(pairs, w_enc, w_dec, far, True, "enc_other")
+    got = swap(send, "narrow", far)
+    mine, squares_own = encode(pairs, w_enc, w_dec, far, False, "enc_own")
+    (pre,) = pointwise(lambda a, b: (a + b,), "pre", [mine, got], [wide_f32], w_dec)
     for bit in near[:-1]:
         pre = pre + swap(pre, "narrow", bit)
     last = swap(pre, "narrow", near[-1])
 
-    def first_codes(a, b, bias):
-        value = jnp.maximum(a + b + bias, 0.0)
-        return value, value.astype(BF16)
-
-    latents, codes = pointwise(first_codes, "latents", [pre, last, b_enc_own], [wide_f32, lat_bf16], w_dec)
-
     half_row = jax.ShapeDtypeStruct((1, lat // 2), F32)
     two_rows = jax.ShapeDtypeStruct((2, lat // 2), F32)
-    norms = squares_of(w_dec, far)
+    (norms,) = pointwise(lambda a, b: (jnp.concatenate([a, b]),), "squares", [squares_own, squares_other], [two_rows], w_dec)
     for bit in near[:-1]:
         (norms,) = pointwise(lambda a, b: (a + b,), "squared", [norms, swap(norms, "narrow", bit)], [two_rows], w_dec)
 
@@ -307,10 +282,16 @@
     norm_own, norm_other = pointwise(roots, "norms", [norms, swap(norms, "narrow", near[-1])], [half_row, half_row], w_dec)
     norm_got = swap(norm_other, "narrow", far)
 
+    def first_codes(a, b, bias, _):
+        value = jnp.maximum(a + b + bias, 0.0)
+        return value, value.astype(BF16)
+
+    latents, codes = pointwise(first_codes, "latents", [pre, last, b_enc_own, norm_other], [wide_f32, lat_bf16], w_dec)
+
     for step in range(ITERS):
         codes_other = swap(codes, "narrow", far)
         acc = product(codes, w_dec, None, F32, lat_own, None, False, f"rebuild_a{step}")
-        send = product(codes_other, w_dec, acc, BF16, lat_other, feat_other, False, f"rebuild_b{step}")
+        send = product(codes_other, w_dec, acc, BF16, lat_other, feat_other, False, f"rebuild_b{step}", after=[norm_got])
         got = swap(send, "wide", hidden)
         mine = product(codes_other, w_dec, acc, F32, lat_other, feat_own, False, f"rebuild_c{step}")
         for bit in open_bits:

time: 124 us -> 110 us (0.89)
  Pallas kernels: 56 us -> 46.1 us
  waiting for transfers between devices: 36.5 us -> 29.7 us
  starting transfers between devices: 27.9 us -> 30.9 us
    pallas_call x34, Pallas kernels: 56 us -> 46.1 us  [local_call(): pl.pallas_call(body, out_shape=outs, in_specs=specs, out_specs=[out_spec]...]
    ppermute x22, waiting for transfers between devices: 36.5 us -> 29.7 us  [swap(): return lax.ppermute(value, axis, pairs)]
    ppermute x22, starting transfers between devices: 27.9 us -> 30.9 us  [swap(): return lax.ppermute(value, axis, pairs)]
  transfers between devices with their start and end apart: 22 -> 22, of which waited for: 18 -> 16; matrix products, arithmetic and copies ran while one was open for 0% -> 0% of each run, Pallas kernels for 31% -> 26%
where the time goes in v2:
time: 110 us
  Pallas kernels  46.1 us (42%)
  starting transfers between devices  30.9 us (28%)
  waiting for transfers between devices  29.7 us (27%)
  local copies, waits for them, and re-layouts  1.62 us (1%)
  between operations  1.61 us (1%)
    pallas_call x34, Pallas kernels, local_call(): pl.pallas_call(body, out_shape=outs, in_specs=specs, out_specs=[out_spec]...  46.1 us
    ppermute x22, starting transfers between devices, swap(): return lax.ppermute(value, axis, pairs)  30.9 us
    ppermute x22, waiting for transfers between devices, swap(): return lax.ppermute(value, axis, pairs)  29.7 us
  transfers between devices with their start and end apart: 22, of which 16 were waited for; matrix products, arithmetic and copies ran while one was open for 0% of the time, Pallas kernels for 26%

profile of v2, /device:TPU:0, one launch (start us, length us, event | category | flops | bytes accessed | tf_op | source)
XLA Modules:
  0.0 110.0 jit_solution(11203453094004764228)
XLA Ops:
  1.3 0.9 copy-done
  2.9 1.1 select.1
  4.0 3.0 %collective-permute-start = (bf16[2,4096]{1,0:T(2,128)(2,1)S(1)}, bf16[2,4096]{1,0:T(2,128)(2,1)S(1)}, u32[]{:S(2)}, u32[]{:S(2)}) collective-permute-start(bf16[2,4096]{1,0:T(2,128)(2,1)S(1)} %get-tuple-element.25.mine_ref), channel_id=1, source_target_pairs={{0,4},{4,0},{8,12},{12,8},{16,20},{20,16},{24,28},{28,24},{1,5},{5... | collective-permute-start | bytes 49160 | tf_op jit(solution)/shard_map/ppermute | solution.py:19
  7.0 1.7 %collective-permute-done.other_ref = bf16[2,4096]{1,0:T(2,128)(2,1)S(1)} collective-permute-done((bf16[2,4096]{1,0:T(2,128)(2,1)S(1)}, bf16[2,4096]{1,0:T(2,128)(2,1)S(1)}, u32[]{:S(2)}, u32[]{:S(2)}) %collective-permute-start) | collective-permute-done | bytes 16416 | tf_op jit(solution)/shard_map/ppermute | solution.py:19
  8.8 2.2 %collective-permute-start.1 = (bf16[4,4096]{1,0:T(4,128)(2,1)S(1)}, bf16[4,4096]{1,0:T(4,128)(2,1)S(1)}, u32[]{:S(2)}, u32[]{:S(2)}) collective-permute-start(bf16[4,4096]{1,0:T(4,128)(2,1)S(1)} %merge.2.mine_ref), channel_id=1, source_target_pairs={{0,8},{4,12},{8,0},{12,4},{16,24},{20,28},{24,16},{28,20},{1,9},{5... | collective-permute-start | bytes 98312 | tf_op jit(solution)/shard_map/ppermute | solution.py:19
  11.0 1.9 %collective-permute-done.1.other_ref = bf16[4,4096]{1,0:T(4,128)(2,1)S(1)} collective-permute-done((bf16[4,4096]{1,0:T(4,128)(2,1)S(1)}, bf16[4,4096]{1,0:T(4,128)(2,1)S(1)}, u32[]{:S(2)}, u32[]{:S(2)}) %collective-permute-start.1) | collective-permute-done | bytes 32800 | tf_op jit(solution)/shard_map/ppermute | solution.py:19
  12.9 3.1 %collective-permute-start.2 = (bf16[8,4096]{1,0:T(8,128)(2,1)S(1)}, bf16[8,4096]{1,0:T(8,128)(2,1)S(1)}, u32[]{:S(2)}, u32[]{:S(2)}) collective-permute-start(bf16[8,4096]{1,0:T(8,128)(2,1)S(1)} %merge.3.mine_ref), channel_id=1, source_target_pairs={{0,16},{4,20},{8,24},{12,28},{16,0},{20,4},{24,8},{28,12},{1,17},{... | collective-permute-start | bytes 196616 | tf_op jit(solution)/shard_map/ppermute | solution.py:19
  16.1 2.2 %collective-permute-done.2.other_ref = bf16[8,4096]{1,0:T(8,128)(2,1)S(1)} collective-permute-done((bf16[8,4096]{1,0:T(8,128)(2,1)S(1)}, bf16[8,4096]{1,0:T(8,128)(2,1)S(1)}, u32[]{:S(2)}, u32[]{:S(2)}) %collective-permute-start.2) | collective-permute-done | bytes 65568 | tf_op jit(solution)/shard_map/ppermute | solution.py:19
  18.9 6.5 %enc_other.1 = (f32[16,2048]{1,0:T(8,128)S(1)}, f32[1,2048]{1,0:T(1,128)S(1)}) custom-call(bf16[16,4096]{1,0:T(8,128)(2,1)S(1)} %get-tuple-element.28.x_ref, bf16[4096,4096]{1,0:T(8,128)(2,1)} %w_ref.17, bf16[4096,4096]{1,0:T(8,128)(2,1)S(1)} %bitcast.7), custom_call_target="tpu_custom_call" | custom-call | flops 268435456 | bytes 8388608 | tf_op jit(solution)/shard_map/enc_other/pallas_call | solution.py:46
  25.4 1.9 %collective-permute-start.3 = (f32[16,2048]{1,0:T(8,128)S(1)}, f32[16,2048]{1,0:T(8,128)S(1)}, u32[]{:S(2)}, u32[]{:S(2)}) collective-permute-start(f32[16,2048]{1,0:T(8,128)S(1)} %get-tuple-element.30), channel_id=1, source_target_pairs={{0,2},{1,3},{2,0},{3,1},{4,6},{5,7},{6,4},{7,5},{8,10},{9,11},{10,... | collective-permute-start | bytes 393224 | tf_op jit(solution)/shard_map/ppermute | solution.py:19
  27.3 6.5 %enc_own.1 = (f32[16,2048]{1,0:T(8,128)S(1)}, f32[1,2048]{1,0:T(1,128)S(1)}) custom-call(bf16[16,4096]{1,0:T(8,128)(2,1)S(1)} %get-tuple-element.28.x_ref, bf16[4096,4096]{1,0:T(8,128)(2,1)} %w_ref.17, bf16[4096,4096]{1,0:T(8,128)(2,1)S(1)} %bitcast.7), custom_call_target="tpu_custom_call" | custom-call | flops 268435456 | bytes 8388608 | tf_op jit(solution)/shard_map/enc_own/pallas_call | solution.py:46
  34.6 0.8 collective-permute-done.5.refs_1_
  35.7 1.8 %collective-permute-start.7 = (f32[1,2048]{1,0:T(1,128)S(1)}, f32[1,2048]{1,0:T(1,128)S(1)}, u32[]{:S(2)}, u32[]{:S(2)}) collective-permute-start(f32[1,2048]{1,0:T(1,128)S(1)} %get-tuple-element.34.refs_3_), channel_id=1, source_target_pairs={{0,2},{1,3},{2,0},{3,1},{4,6},{5,7},{6,4},{7,5},{8,10},{9,11},{10,... | collective-permute-start | bytes 24584 | tf_op jit(solution)/shard_map/ppermute | solution.py:19
  37.6 2.6 %rebuild_a0.1.rest_0_ = f32[16,4096]{1,0:T(8,128)S(1)} custom-call(bf16[16,2048]{1,0:T(8,128)(2,1)S(1)} %get-tuple-element.36.x_ref, bf16[4096,4096]{1,0:T(8,128)(2,1)S(1)} %bitcast.7), custom_call_target="tpu_custom_call" | custom-call | flops 268435456 | bytes 8388608 | tf_op jit(solution)/shard_map/rebuild_a0/pallas_call | solution.py:46
  40.2 1.3 %rebuild_b0.1 = bf16[16,2048]{1,0:T(8,128)(2,1)S(1)} custom-call(bf16[16,2048]{1,0:T(8,128)(2,1)S(1)} %collective-permute-done.6.x_ref, bf16[4096,4096]{1,0:T(8,128)(2,1)S(1)} %bitcast.7, f32[16,4096]{1,0:T(8,128)S(1)} %rebuild_a0.1.rest_0_, f32[1,2048]{1,0:T(1,128)S(1)} %collective-permute-done.7.rest_1_.refs_6_), custom_call_target="tpu_custom_call" | custom-call | flops 134217728 | bytes 4194304 | tf_op jit(solution)/shard_map/rebuild_b0/pallas_call | solution.py:46
  41.5 1.5 %collective-permute-start.8 = (bf16[16,2048]{1,0:T(8,128)(2,1)S(1)}, bf16[16,2048]{1,0:T(8,128)(2,1)S(1)}, u32[]{:S(2)}, u32[]{:S(2)}) collective-permute-start(bf16[16,2048]{1,0:T(8,128)(2,1)S(1)} %rebuild_b0.1), channel_id=1, source_target_pairs={{0,4},{4,0},{8,12},{12,8},{16,20},{20,16},{24,28},{28,24},{1,5},{5... | collective-permute-start | bytes 196616 | tf_op jit(solution)/shard_map/ppermute | solution.py:19
  43.0 1.3 %rebuild_c0.1.refs_0_ = f32[16,2048]{1,0:T(8,128)S(1)} custom-call(bf16[16,2048]{1,0:T(8,128)(2,1)S(1)} %collective-permute-done.6.x_ref, bf16[4096,4096]{1,0:T(8,128)(2,1)S(1)} %bitcast.7, f32[16,4096]{1,0:T(8,128)S(1)} %rebuild_a0.1.rest_0_), custom_call_target="tpu_custom_call" | custom-call | flops 134217728 | bytes 4194304 | tf_op jit(solution)/shard_map/rebuild_c0/pallas_call | solution.py:46
  44.3 1.5 %collective-permute-done.8.refs_1_ = bf16[16,2048]{1,0:T(8,128)(2,1)S(1)} collective-permute-done((bf16[16,2048]{1,0:T(8,128)(2,1)S(1)}, bf16[16,2048]{1,0:T(8,128)(2,1)S(1)}, u32[]{:S(2)}, u32[]{:S(2)}) %collective-permute-start.8) | collective-permute-done | bytes 65568 | tf_op jit(solution)/shard_map/ppermute | solution.py:19
  45.8 1.6 %collective-permute-start.9 = (bf16[16,2048]{1,0:T(8,128)(2,1)S(1)}, bf16[16,2048]{1,0:T(8,128)(2,1)S(1)}, u32[]{:S(2)}, u32[]{:S(2)}) collective-permute-start(bf16[16,2048]{1,0:T(8,128)(2,1)S(1)} %rebuilt0.2.refs_0_), channel_id=1, source_target_pairs={{0,8},{4,12},{8,0},{12,4},{16,24},{20,28},{24,16},{28,20},{1,9},{5... | collective-permute-start | bytes 196616 | tf_op jit(solution)/shard_map/ppermute | solution.py:19
  47.5 2.7 %collective-permute-done.9.refs_1_ = bf16[16,2048]{1,0:T(8,128)(2,1)S(1)} collective-permute-done((bf16[16,2048]{1,0:T(8,128)(2,1)S(1)}, bf16[16,2048]{1,0:T(8,128)(2,1)S(1)}, u32[]{:S(2)}, u32[]{:S(2)}) %collective-permute-start.9) | collective-permute-done | bytes 65568 | tf_op jit(solution)/shard_map/ppermute | solution.py:19
  50.2 2.8 %collective-permute-start.10 = (bf16[16,2048]{1,0:T(8,128)(2,1)S(1)}, bf16[16,2048]{1,0:T(8,128)(2,1)S(1)}, u32[]{:S(2)}, u32[]{:S(2)}) collective-permute-start(bf16[16,2048]{1,0:T(8,128)(2,1)S(1)} %rebuilt0.3.refs_0_), channel_id=1, source_target_pairs={{0,16},{4,20},{8,24},{12,28},{16,0},{20,4},{24,8},{28,12},{1,17},{... | collective-permute-start | bytes 196616 | tf_op jit(solution)/shard_map/ppermute | solution.py:19
  53.0 2.4 %collective-permute-done.10.refs_1_ = bf16[16,2048]{1,0:T(8,128)(2,1)S(1)} collective-permute-done((bf16[16,2048]{1,0:T(8,128)(2,1)S(1)}, bf16[16,2048]{1,0:T(8,128)(2,1)S(1)}, u32[]{:S(2)}, u32[]{:S(2)}) %collective-permute-start.10) | collective-permute-done | bytes 65568 | tf_op jit(solution)/shard_map/ppermute | solution.py:19
  55.4 1.6 %collective-permute-start.11 = (bf16[16,2048]{1,0:T(8,128)(2,1)S(1)}, bf16[16,2048]{1,0:T(8,128)(2,1)S(1)}, u32[]{:S(2)}, u32[]{:S(2)}) collective-permute-start(bf16[16,2048]{1,0:T(8,128)(2,1)S(1)} %residual0.1.x_ref), channel_id=1, source_target_pairs={{0,4},{4,0},{8,12},{12,8},{16,20},{20,16},{24,28},{28,24},{1,5},{5... | collective-permute-start | bytes 196616 | tf_op jit(solution)/shard_map/ppermute | solution.py:19
  57.0 4.8 %grad_a0.1.rest_0_ = f32[16,4096]{1,0:T(8,128)S(1)} custom-call(bf16[16,2048]{1,0:T(8,128)(2,1)S(1)} %residual0.1.x_ref, bf16[4096,4096]{1,0:T(8,128)(2,1)S(1)} %bitcast.7), custom_call_target="tpu_custom_call" | custom-call | flops 268435456 | bytes 8388608 | tf_op jit(solution)/shard_map/grad_a0/pallas_call | solution.py:46
  61.8 2.4 %grad_b0.1 = bf16[16,2048]{1,0:T(8,128)(2,1)S(1)} custom-call(bf16[16,2048]{1,0:T(8,128)(2,1)S(1)} %collective-permute-done.11.x_ref, bf16[4096,4096]{1,0:T(8,128)(2,1)S(1)} %bitcast.7, f32[16,4096]{1,0:T(8,128)S(1)} %grad_a0.1.rest_0_), custom_call_target="tpu_custom_call" | custom-call | flops 134217728 | bytes 4194304 | tf_op jit(solution)/shard_map/grad_b0/pallas_call | solution.py:46
  64.2 1.0 collective-permute-start.12
  65.2 2.4 %grad_c0.1.refs_0_ = f32[16,2048]{1,0:T(8,128)S(1)} custom-call(bf16[16,2048]{1,0:T(8,128)(2,1)S(1)} %collective-permute-done.11.x_ref, bf16[4096,4096]{1,0:T(8,128)(2,1)S(1)} %bitcast.7, f32[16,4096]{1,0:T(8,128)S(1)} %grad_a0.1.rest_0_), custom_call_target="tpu_custom_call" | custom-call | flops 134217728 | bytes 4194304 | tf_op jit(solution)/shard_map/grad_c0/pallas_call | solution.py:46
  67.6 0.9 collective-permute-done.12.refs_1_
  68.6 1.3 %collective-permute-done.13.refs_2_ = f32[16,2048]{1,0:T(8,128)S(1)} collective-permute-done((f32[16,2048]{1,0:T(8,128)S(1)}, f32[16,2048]{1,0:T(8,128)S(1)}, u32[]{:S(2)}, u32[]{:S(2)}) %collective-permute-start.13) | collective-permute-done | bytes 131104 | tf_op jit(solution)/shard_map/ppermute | solution.py:19
  69.9 1.1 collective-permute-start.14
  71.0 2.6 %rebuild_a1.1.rest_0_ = f32[16,4096]{1,0:T(8,128)S(1)} custom-call(bf16[16,2048]{1,0:T(8,128)(2,1)S(1)} %get-tuple-element.43.x_ref, bf16[4096,4096]{1,0:T(8,128)(2,1)S(1)} %bitcast.7), custom_call_target="tpu_custom_call" | custom-call | flops 268435456 | bytes 8388608 | tf_op jit(solution)/shard_map/rebuild_a1/pallas_call | solution.py:46
  74.3 1.3 %rebuild_b1.1 = bf16[16,2048]{1,0:T(8,128)(2,1)S(1)} custom-call(bf16[16,2048]{1,0:T(8,128)(2,1)S(1)} %collective-permute-done.14.x_ref, bf16[4096,4096]{1,0:T(8,128)(2,1)S(1)} %bitcast.7, f32[16,4096]{1,0:T(8,128)S(1)} %rebuild_a1.1.rest_0_, f32[1,2048]{1,0:T(1,128)S(1)} %collective-permute-done.7.rest_1_.refs_6_), custom_call_target="tpu_custom_call" | custom-call | flops 134217728 | bytes 4194304 | tf_op jit(solution)/shard_map/rebuild_b1/pallas_call | solution.py:46
  76.1 1.3 %rebuild_c1.1.refs_0_ = f32[16,2048]{1,0:T(8,128)S(1)} custom-call(bf16[16,2048]{1,0:T(8,128)(2,1)S(1)} %collective-permute-done.14.x_ref, bf16[4096,4096]{1,0:T(8,128)(2,1)S(1)} %bitcast.7, f32[16,4096]{1,0:T(8,128)S(1)} %rebuild_a1.1.rest_0_), custom_call_target="tpu_custom_call" | custom-call | flops 134217728 | bytes 4194304 | tf_op jit(solution)/shard_map/rebuild_c1/pallas_call | solution.py:46
  77.5 2.4 %collective-permute-done.15.refs_1_ = bf16[16,2048]{1,0:T(8,128)(2,1)S(1)} collective-permute-done((bf16[16,2048]{1,0:T(8,128)(2,1)S(1)}, bf16[16,2048]{1,0:T(8,128)(2,1)S(1)}, u32[]{:S(2)}, u32[]{:S(2)}) %collective-permute-start.15) | collective-permute-done | bytes 65568 | tf_op jit(solution)/shard_map/ppermute | solution.py:19
  79.9 1.9 %collective-permute-start.16 = (bf16[16,2048]{1,0:T(8,128)(2,1)S(1)}, bf16[16,2048]{1,0:T(8,128)(2,1)S(1)}, u32[]{:S(2)}, u32[]{:S(2)}) collective-permute-start(bf16[16,2048]{1,0:T(8,128)(2,1)S(1)} %rebuilt1.2.refs_0_), channel_id=1, source_target_pairs={{0,8},{4,12},{8,0},{12,4},{16,24},{20,28},{24,16},{28,20},{1,9},{5... | collective-permute-start | bytes 196616 | tf_op jit(solution)/shard_map/ppermute | solution.py:19
  81.8 2.4 %collective-permute-done.16.refs_1_ = bf16[16,2048]{1,0:T(8,128)(2,1)S(1)} collective-permute-done((bf16[16,2048]{1,0:T(8,128)(2,1)S(1)}, bf16[16,2048]{1,0:T(8,128)(2,1)S(1)}, u32[]{:S(2)}, u32[]{:S(2)}) %collective-permute-start.16) | collective-permute-done | bytes 65568 | tf_op jit(solution)/shard_map/ppermute | solution.py:19
  84.2 3.0 %collective-permute-start.17 = (bf16[16,2048]{1,0:T(8,128)(2,1)S(1)}, bf16[16,2048]{1,0:T(8,128)(2,1)S(1)}, u32[]{:S(2)}, u32[]{:S(2)}) collective-permute-start(bf16[16,2048]{1,0:T(8,128)(2,1)S(1)} %rebuilt1.3.refs_0_), channel_id=1, source_target_pairs={{0,16},{4,20},{8,24},{12,28},{16,0},{20,4},{24,8},{28,12},{1,17},{... | collective-permute-start | bytes 196616 | tf_op jit(solution)/shard_map/ppermute | solution.py:19
  87.2 2.2 %collective-permute-done.17.refs_1_ = bf16[16,2048]{1,0:T(8,128)(2,1)S(1)} collective-permute-done((bf16[16,2048]{1,0:T(8,128)(2,1)S(1)}, bf16[16,2048]{1,0:T(8,128)(2,1)S(1)}, u32[]{:S(2)}, u32[]{:S(2)}) %collective-permute-start.17) | collective-permute-done | bytes 65568 | tf_op jit(solution)/shard_map/ppermute | solution.py:19
  90.1 4.8 %grad_a1.1.rest_0_ = f32[16,4096]{1,0:T(8,128)S(1)} custom-call(bf16[16,2048]{1,0:T(8,128)(2,1)S(1)} %residual1.1.x_ref, bf16[4096,4096]{1,0:T(8,128)(2,1)S(1)} %bitcast.7), custom_call_target="tpu_custom_call" | custom-call | flops 268435456 | bytes 8388608 | tf_op jit(solution)/shard_map/grad_a1/pallas_call | solution.py:46
  94.9 2.4 %grad_b1.1 = bf16[16,2048]{1,0:T(8,128)(2,1)S(1)} custom-call(bf16[16,2048]{1,0:T(8,128)(2,1)S(1)} %collective-permute-done.18.x_ref, bf16[4096,4096]{1,0:T(8,128)(2,1)S(1)} %bitcast.7, f32[16,4096]{1,0:T(8,128)S(1)} %grad_a1.1.rest_0_), custom_call_target="tpu_custom_call" | custom-call | flops 134217728 | bytes 4194304 | tf_op jit(solution)/shard_map/grad_b1/pallas_call | solution.py:46
  97.3 1.1 %collective-permute-start.19 = (bf16[16,2048]{1,0:T(8,128)(2,1)S(1)}, bf16[16,2048]{1,0:T(8,128)(2,1)S(1)}, u32[]{:S(2)}, u32[]{:S(2)}) collective-permute-start(bf16[16,2048]{1,0:T(8,128)(2,1)S(1)} %grad_b1.1), channel_id=1, source_target_pairs={{0,2},{1,3},{2,0},{3,1},{4,6},{5,7},{6,4},{7,5},{8,10},{9,11},{10,... | collective-permute-start | bytes 196616 | tf_op jit(solution)/shard_map/ppermute | solution.py:19
  98.4 2.4 %grad_c1.1.refs_0_ = f32[16,2048]{1,0:T(8,128)S(1)} custom-call(bf16[16,2048]{1,0:T(8,128)(2,1)S(1)} %collective-permute-done.18.x_ref, bf16[4096,4096]{1,0:T(8,128)(2,1)S(1)} %bitcast.7, f32[16,4096]{1,0:T(8,128)S(1)} %grad_a1.1.rest_0_), custom_call_target="tpu_custom_call" | custom-call | flops 134217728 | bytes 4194304 | tf_op jit(solution)/shard_map/grad_c1/pallas_call | solution.py:46
  100.8 0.8 collective-permute-done.19.refs_1_
  101.7 1.3 %collective-permute-done.20.refs_2_ = f32[16,2048]{1,0:T(8,128)S(1)} collective-permute-done((f32[16,2048]{1,0:T(8,128)S(1)}, f32[16,2048]{1,0:T(8,128)S(1)}, u32[]{:S(2)}, u32[]{:S(2)}) %collective-permute-start.20) | collective-permute-done | bytes 131104 | tf_op jit(solution)/shard_map/ppermute | solution.py:19
  103.0 0.7 update1.1
  103.7 1.1 %collective-permute-start.21 = (f32[16,2048]{1,0:T(8,128)S(1)}, f32[16,2048]{1,0:T(8,128)S(1)}, u32[]{:S(2)}, u32[]{:S(2)}) collective-permute-start(f32[16,2048]{1,0:T(8,128)S(1)} %get-tuple-element.44.own_ref), channel_id=1, source_target_pairs={{0,2},{1,3},{2,0},{3,1},{4,6},{5,7},{6,4},{7,5},{8,10},{9,11},{10,... | collective-permute-start | bytes 393224 | tf_op jit(solution)/shard_map/ppermute | solution.py:19
  104.8 4.4 %collective-permute-done.21.other_ref = f32[16,2048]{1,0:T(8,128)S(1)} collective-permute-done((f32[16,2048]{1,0:T(8,128)S(1)}, f32[16,2048]{1,0:T(8,128)S(1)}, u32[]{:S(2)}, u32[]{:S(2)}) %collective-permute-start.21) | collective-permute-done | bytes 131104 | tf_op jit(solution)/shard_map/ppermute | solution.py:19
  109.2 0.7 finish.1
  (59 shorter events, 4.5 us)
Async XLA Ops:
  1.3 0.9 copy-start
  2.2 0.7 copy-start.5
  3.9 9.0 %copy-start.1 = (f32[1,2048]{1,0:T(1,128)}, f32[1,2048]{1,0:T(1,128)S(1)}, u32[]{:S(2)}) copy-start(f32[1,2048]{1,0:T(1,128)S(1)} %get-tuple-element.27.after_ref.pen_ref) | copy-start | bytes 24580
  3.9 12.1 %slice-start = ((s8[33554432]{0:T(1024)(128)(4,1)}), s8[4194304]{0:T(1024)(128)(4,1)S(1)}, s32[]{:S(2)}) async-start(s8[33554432]{0:T(1024)(128)(4,1)} %bitcast.6), calls=%async_computation | async-start | bytes 8388608
  3.9 12.1 %slice-start.1 = ((s8[33554432]{0:T(1024)(128)(4,1)}), s8[4194304]{0:T(1024)(128)(4,1)S(1)}, s32[]{:S(2)}) async-start(s8[33554432]{0:T(1024)(128)(4,1)} %bitcast.6), calls=%async_computation.1 | async-start | bytes 8388608
  3.9 12.1 %slice-start.2 = ((s8[33554432]{0:T(1024)(128)(4,1)}), s8[4194304]{0:T(1024)(128)(4,1)S(1)}, s32[]{:S(2)}) async-start(s8[33554432]{0:T(1024)(128)(4,1)} %bitcast.6), calls=%async_computation.2 | async-start | bytes 8388608
  4.0 12.1 %slice-start.3 = ((s8[33554432]{0:T(1024)(128)(4,1)}), s8[4194304]{0:T(1024)(128)(4,1)S(1)}, s32[]{:S(2)}) async-start(s8[33554432]{0:T(1024)(128)(4,1)} %bitcast.6), calls=%async_computation.3 | async-start | bytes 8388608
  4.0 4.8 %collective-permute-start = (bf16[2,4096]{1,0:T(2,128)(2,1)S(1)}, bf16[2,4096]{1,0:T(2,128)(2,1)S(1)}, u32[]{:S(2)}, u32[]{:S(2)}) collective-permute-start(bf16[2,4096]{1,0:T(2,128)(2,1)S(1)} %get-tuple-element.25.mine_ref), channel_id=1, source_target_pairs={{0,4},{4,0},{8,12},{12,8},{16,20},{20,16},{24,28},{28,24},{1,5},{5... | collective-permute-start | bytes 49160 | tf_op jit(solution)/shard_map/ppermute | solution.py:19
  8.8 7.3 %slice-start.4 = ((s8[33554432]{0:T(1024)(128)(4,1)}), s8[4194304]{0:T(1024)(128)(4,1)S(1)}, s32[]{:S(2)}) async-start(s8[33554432]{0:T(1024)(128)(4,1)} %bitcast.6), calls=%async_computation.4 | async-start | bytes 8388608
  8.8 7.3 %slice-start.5 = ((s8[33554432]{0:T(1024)(128)(4,1)}), s8[4194304]{0:T(1024)(128)(4,1)S(1)}, s32[]{:S(2)}) async-start(s8[33554432]{0:T(1024)(128)(4,1)} %bitcast.6), calls=%async_computation.5 | async-start | bytes 8388608
  8.8 7.3 %slice-start.6 = ((s8[33554432]{0:T(1024)(128)(4,1)}), s8[4194304]{0:T(1024)(128)(4,1)S(1)}, s32[]{:S(2)}) async-start(s8[33554432]{0:T(1024)(128)(4,1)} %bitcast.6), calls=%async_computation.6 | async-start | bytes 8388608
  8.8 7.3 %slice-start.7 = ((s8[33554432]{0:T(1024)(128)(4,1)}), s8[4194304]{0:T(1024)(128)(4,1)S(1)}, s32[]{:S(2)}) async-start(s8[33554432]{0:T(1024)(128)(4,1)} %bitcast.6), calls=%async_computation.7 | async-start | bytes 8388608
  8.8 9.5 %copy-start.3 = (f32[4096]{0:T(1024)S(1)}, f32[4096]{0:T(1024)}, u32[]{:S(2)}) copy-start(f32[4096]{0:T(1024)} %param.11) | copy-start | bytes 49156
  8.8 9.5 %copy-start.4 = (f32[4096]{0:T(1024)S(1)}, f32[4096]{0:T(1024)}, u32[]{:S(2)}) copy-start(f32[4096]{0:T(1024)} %param.13) | copy-start | bytes 49156
  8.8 4.1 %collective-permute-start.1 = (bf16[4,4096]{1,0:T(4,128)(2,1)S(1)}, bf16[4,4096]{1,0:T(4,128)(2,1)S(1)}, u32[]{:S(2)}, u32[]{:S(2)}) collective-permute-start(bf16[4,4096]{1,0:T(4,128)(2,1)S(1)} %merge.2.mine_ref), channel_id=1, source_target_pairs={{0,8},{4,12},{8,0},{12,4},{16,24},{20,28},{24,16},{28,20},{1,9},{5... | collective-permute-start | bytes 98312 | tf_op jit(solution)/shard_map/ppermute | solution.py:19
  12.9 5.3 %collective-permute-start.2 = (bf16[8,4096]{1,0:T(8,128)(2,1)S(1)}, bf16[8,4096]{1,0:T(8,128)(2,1)S(1)}, u32[]{:S(2)}, u32[]{:S(2)}) collective-permute-start(bf16[8,4096]{1,0:T(8,128)(2,1)S(1)} %merge.3.mine_ref), channel_id=1, source_target_pairs={{0,16},{4,20},{8,24},{12,28},{16,0},{20,4},{24,8},{28,12},{1,17},{... | collective-permute-start | bytes 196616 | tf_op jit(solution)/shard_map/ppermute | solution.py:19
  16.0 2.3 %copy-start.2 = (f32[1,2048]{1,0:T(1,128)S(1)}, f32[1,2048]{1,0:T(1,128)}, u32[]{:S(2)}) copy-start(f32[1,2048]{1,0:T(1,128)} %copy-done.1) | copy-start | bytes 24580
  25.4 8.4 %collective-permute-start.3 = (f32[16,2048]{1,0:T(8,128)S(1)}, f32[16,2048]{1,0:T(8,128)S(1)}, u32[]{:S(2)}, u32[]{:S(2)}) collective-permute-start(f32[16,2048]{1,0:T(8,128)S(1)} %get-tuple-element.30), channel_id=1, source_target_pairs={{0,2},{1,3},{2,0},{3,1},{4,6},{5,7},{6,4},{7,5},{8,10},{9,11},{10,... | collective-permute-start | bytes 393224 | tf_op jit(solution)/shard_map/ppermute | solution.py:19
  33.9 1.5 %collective-permute-start.4 = (f32[16,2048]{1,0:T(8,128)S(1)}, f32[16,2048]{1,0:T(8,128)S(1)}, u32[]{:S(2)}, u32[]{:S(2)}) collective-permute-start(f32[16,2048]{1,0:T(8,128)S(1)} %pre.1.refs_0_), channel_id=1, source_target_pairs={{0,1},{1,0},{2,3},{3,2},{4,5},{5,4},{6,7},{7,6},{8,9},{9,8},{10,11... | collective-permute-start | bytes 393224 | tf_op jit(solution)/shard_map/ppermute | solution.py:19
  34.0 1.4 %collective-permute-start.5 = (f32[2,2048]{1,0:T(2,128)S(1)}, f32[2,2048]{1,0:T(2,128)S(1)}, u32[]{:S(2)}, u32[]{:S(2)}) collective-permute-start(f32[2,2048]{1,0:T(2,128)S(1)} %squares.1.refs_0_), channel_id=1, source_target_pairs={{0,1},{1,0},{2,3},{3,2},{4,5},{5,4},{6,7},{7,6},{8,9},{9,8},{10,11... | collective-permute-start | bytes 49160 | tf_op jit(solution)/shard_map/ppermute | solution.py:19
  35.5 4.7 %collective-permute-start.6 = (bf16[16,2048]{1,0:T(8,128)(2,1)S(1)}, bf16[16,2048]{1,0:T(8,128)(2,1)S(1)}, u32[]{:S(2)}, u32[]{:S(2)}) collective-permute-start(bf16[16,2048]{1,0:T(8,128)(2,1)S(1)} %get-tuple-element.36.x_ref), channel_id=1, source_target_pairs={{0,2},{1,3},{2,0},{3,1},{4,6},{5,7},{6,4},{7,5},{8,10},{9,11},{10,... | collective-permute-start | bytes 196616 | tf_op jit(solution)/shard_map/ppermute | solution.py:19
  35.7 4.5 %collective-permute-start.7 = (f32[1,2048]{1,0:T(1,128)S(1)}, f32[1,2048]{1,0:T(1,128)S(1)}, u32[]{:S(2)}, u32[]{:S(2)}) collective-permute-start(f32[1,2048]{1,0:T(1,128)S(1)} %get-tuple-element.34.refs_3_), channel_id=1, source_target_pairs={{0,2},{1,3},{2,0},{3,1},{4,6},{5,7},{6,4},{7,5},{8,10},{9,11},{10,... | collective-permute-start | bytes 24584 | tf_op jit(solution)/shard_map/ppermute | solution.py:19
  41.5 4.3 %collective-permute-start.8 = (bf16[16,2048]{1,0:T(8,128)(2,1)S(1)}, bf16[16,2048]{1,0:T(8,128)(2,1)S(1)}, u32[]{:S(2)}, u32[]{:S(2)}) collective-permute-start(bf16[16,2048]{1,0:T(8,128)(2,1)S(1)} %rebuild_b0.1), channel_id=1, source_target_pairs={{0,4},{4,0},{8,12},{12,8},{16,20},{20,16},{24,28},{28,24},{1,5},{5... | collective-permute-start | bytes 196616 | tf_op jit(solution)/shard_map/ppermute | solution.py:19
  45.8 4.3 %collective-permute-start.9 = (bf16[16,2048]{1,0:T(8,128)(2,1)S(1)}, bf16[16,2048]{1,0:T(8,128)(2,1)S(1)}, u32[]{:S(2)}, u32[]{:S(2)}) collective-permute-start(bf16[16,2048]{1,0:T(8,128)(2,1)S(1)} %rebuilt0.2.refs_0_), channel_id=1, source_target_pairs={{0,8},{4,12},{8,0},{12,4},{16,24},{20,28},{24,16},{28,20},{1,9},{5... | collective-permute-start | bytes 196616 | tf_op jit(solution)/shard_map/ppermute | solution.py:19
  50.2 5.2 %collective-permute-start.10 = (bf16[16,2048]{1,0:T(8,128)(2,1)S(1)}, bf16[16,2048]{1,0:T(8,128)(2,1)S(1)}, u32[]{:S(2)}, u32[]{:S(2)}) collective-permute-start(bf16[16,2048]{1,0:T(8,128)(2,1)S(1)} %rebuilt0.3.refs_0_), channel_id=1, source_target_pairs={{0,16},{4,20},{8,24},{12,28},{16,0},{20,4},{24,8},{28,12},{1,17},{... | collective-permute-start | bytes 196616 | tf_op jit(solution)/shard_map/ppermute | solution.py:19
  55.4 6.3 %collective-permute-start.11 = (bf16[16,2048]{1,0:T(8,128)(2,1)S(1)}, bf16[16,2048]{1,0:T(8,128)(2,1)S(1)}, u32[]{:S(2)}, u32[]{:S(2)}) collective-permute-start(bf16[16,2048]{1,0:T(8,128)(2,1)S(1)} %residual0.1.x_ref), channel_id=1, source_target_pairs={{0,4},{4,0},{8,12},{12,8},{16,20},{20,16},{24,28},{28,24},{1,5},{5... | collective-permute-start | bytes 196616 | tf_op jit(solution)/shard_map/ppermute | solution.py:19
  64.2 4.3 %collective-permute-start.12 = (bf16[16,2048]{1,0:T(8,128)(2,1)S(1)}, bf16[16,2048]{1,0:T(8,128)(2,1)S(1)}, u32[]{:S(2)}, u32[]{:S(2)}) collective-permute-start(bf16[16,2048]{1,0:T(8,128)(2,1)S(1)} %grad_b0.1), channel_id=1, source_target_pairs={{0,2},{1,3},{2,0},{3,1},{4,6},{5,7},{6,4},{7,5},{8,10},{9,11},{10,... | collective-permute-start | bytes 196616 | tf_op jit(solution)/shard_map/ppermute | solution.py:19
  68.5 1.4 %collective-permute-start.13 = (f32[16,2048]{1,0:T(8,128)S(1)}, f32[16,2048]{1,0:T(8,128)S(1)}, u32[]{:S(2)}, u32[]{:S(2)}) collective-permute-start(f32[16,2048]{1,0:T(8,128)S(1)} %grad0.1.refs_1_), channel_id=1, source_target_pairs={{0,1},{1,0},{2,3},{3,2},{4,5},{5,4},{6,7},{7,6},{8,9},{9,8},{10,11... | collective-permute-start | bytes 393224 | tf_op jit(solution)/shard_map/ppermute | solution.py:19
  69.9 4.3 %collective-permute-start.14 = (bf16[16,2048]{1,0:T(8,128)(2,1)S(1)}, bf16[16,2048]{1,0:T(8,128)(2,1)S(1)}, u32[]{:S(2)}, u32[]{:S(2)}) collective-permute-start(bf16[16,2048]{1,0:T(8,128)(2,1)S(1)} %get-tuple-element.43.x_ref), channel_id=1, source_target_pairs={{0,2},{1,3},{2,0},{3,1},{4,6},{5,7},{6,4},{7,5},{8,10},{9,11},{10,... | collective-permute-start | bytes 196616 | tf_op jit(solution)/shard_map/ppermute | solution.py:19
  75.6 4.3 %collective-permute-start.15 = (bf16[16,2048]{1,0:T(8,128)(2,1)S(1)}, bf16[16,2048]{1,0:T(8,128)(2,1)S(1)}, u32[]{:S(2)}, u32[]{:S(2)}) collective-permute-start(bf16[16,2048]{1,0:T(8,128)(2,1)S(1)} %rebuild_b1.1), channel_id=1, source_target_pairs={{0,4},{4,0},{8,12},{12,8},{16,20},{20,16},{24,28},{28,24},{1,5},{5... | collective-permute-start | bytes 196616 | tf_op jit(solution)/shard_map/ppermute | solution.py:19
  79.9 4.3 %collective-permute-start.16 = (bf16[16,2048]{1,0:T(8,128)(2,1)S(1)}, bf16[16,2048]{1,0:T(8,128)(2,1)S(1)}, u32[]{:S(2)}, u32[]{:S(2)}) collective-permute-start(bf16[16,2048]{1,0:T(8,128)(2,1)S(1)} %rebuilt1.2.refs_0_), channel_id=1, source_target_pairs={{0,8},{4,12},{8,0},{12,4},{16,24},{20,28},{24,16},{28,20},{1,9},{5... | collective-permute-start | bytes 196616 | tf_op jit(solution)/shard_map/ppermute | solution.py:19
  84.2 5.2 %collective-permute-start.17 = (bf16[16,2048]{1,0:T(8,128)(2,1)S(1)}, bf16[16,2048]{1,0:T(8,128)(2,1)S(1)}, u32[]{:S(2)}, u32[]{:S(2)}) collective-permute-start(bf16[16,2048]{1,0:T(8,128)(2,1)S(1)} %rebuilt1.3.refs_0_), channel_id=1, source_target_pairs={{0,16},{4,20},{8,24},{12,28},{16,0},{20,4},{24,8},{28,12},{1,17},{... | collective-permute-start | bytes 196616 | tf_op jit(solution)/shard_map/ppermute | solution.py:19
  89.5 5.4 %collective-permute-start.18 = (bf16[16,2048]{1,0:T(8,128)(2,1)S(1)}, bf16[16,2048]{1,0:T(8,128)(2,1)S(1)}, u32[]{:S(2)}, u32[]{:S(2)}) collective-permute-start(bf16[16,2048]{1,0:T(8,128)(2,1)S(1)} %residual1.1.x_ref), channel_id=1, source_target_pairs={{0,4},{4,0},{8,12},{12,8},{16,20},{20,16},{24,28},{28,24},{1,5},{5... | collective-permute-start | bytes 196616 | tf_op jit(solution)/shard_map/ppermute | solution.py:19
  97.3 4.3 %collective-permute-start.19 = (bf16[16,2048]{1,0:T(8,128)(2,1)S(1)}, bf16[16,2048]{1,0:T(8,128)(2,1)S(1)}, u32[]{:S(2)}, u32[]{:S(2)}) collective-permute-start(bf16[16,2048]{1,0:T(8,128)(2,1)S(1)} %grad_b1.1), channel_id=1, source_target_pairs={{0,2},{1,3},{2,0},{3,1},{4,6},{5,7},{6,4},{7,5},{8,10},{9,11},{10,... | collective-permute-start | bytes 196616 | tf_op jit(solution)/shard_map/ppermute | solution.py:19
  101.6 1.4 %collective-permute-start.20 = (f32[16,2048]{1,0:T(8,128)S(1)}, f32[16,2048]{1,0:T(8,128)S(1)}, u32[]{:S(2)}, u32[]{:S(2)}) collective-permute-start(f32[16,2048]{1,0:T(8,128)S(1)} %grad1.1.refs_1_), channel_id=1, source_target_pairs={{0,1},{1,0},{2,3},{3,2},{4,5},{5,4},{6,7},{7,6},{8,9},{9,8},{10,11... | collective-permute-start | bytes 393224 | tf_op jit(solution)/shard_map/ppermute | solution.py:19
  103.7 5.5 %collective-permute-start.21 = (f32[16,2048]{1,0:T(8,128)S(1)}, f32[16,2048]{1,0:T(8,128)S(1)}, u32[]{:S(2)}, u32[]{:S(2)}) collective-permute-start(f32[16,2048]{1,0:T(8,128)S(1)} %get-tuple-element.44.own_ref), channel_id=1, source_target_pairs={{0,2},{1,3},{2,0},{3,1},{4,6},{5,7},{6,4},{7,5},{8,10},{9,11},{10,... | collective-permute-start | bytes 393224 | tf_op jit(solution)/shard_map/ppermute | solution.py:19
